TPU v7x, 256 devices: a whole 4x4x8 slice. The times are simulated.
256 devices in a mesh: first: 16 (over z, core), second: 16 (over y, x).
Axes of the slice: x: 4, y: 4, z: 8, core: 2. Of those that a mesh axis runs over, the one named last changes fastest.
Arguments:
- pair_rows: bfloat16 [768, 768, 128], P('first', 'second'), may hold values from -6 to 6
- in_gain: float32 [128], replicated, may hold values from 0.25 to 1.75
- left_weight: bfloat16 [128, 128], replicated, may hold values from -0.5 to 0.5
- right_weight: bfloat16 [128, 128], replicated, may hold values from -0.5 to 0.5
- mid_gain: float32 [128], replicated, may hold values from 0.25 to 1.75
- out_weight: bfloat16 [128, 128], replicated, may hold values from -0.5 to 0.5
- out_gate: bfloat16 [128, 128], replicated, may hold values from -0.5 to 0.5
Outputs:
- triangle_out: bfloat16 [768, 768, 128], P('first', 'second')
All inputs are finite; a program needn't handle non-finite values.
Results may differ from a plain program's by a relative error of at most 0.012.
Values may be sent and summed in bfloat16 or wider, within the bound.
A program may use at most 64 MiB of HBM per device.

v0:
```python
import jax
import jax.numpy as jnp
from jax import lax
from jax.sharding import PartitionSpec as P


def norm_channels(values, channel_gain):
    centred = values - jnp.mean(values, axis=-1, keepdims=True)
    return (
        centred
        * lax.rsqrt(jnp.mean(centred * centred, axis=-1, keepdims=True) + 1e-05)
        * channel_gain
    )


def project_pair(pair_in, in_gain, left_weight, right_weight):
    ready = norm_channels(pair_in.astype(jnp.float32), in_gain).astype(jnp.bfloat16)
    ready = lax.optimization_barrier(ready)
    left = jnp.einsum("ijc,cd->ijd", ready, left_weight, preferred_element_type=jnp.float32)
    right = jnp.einsum("ijc,cd->ijd", ready, right_weight, preferred_element_type=jnp.float32)
    return (ready, left.astype(jnp.bfloat16), right.astype(jnp.bfloat16))


def to_pair(mixed, ready, mid_gain, out_weight, out_gate):
    scaled = norm_channels(mixed.astype(jnp.float32), mid_gain).astype(jnp.bfloat16)
    scaled = lax.optimization_barrier(scaled)
    gate = jax.nn.sigmoid(
        jnp.einsum("ijc,cd->ijd", ready, out_gate, preferred_element_type=jnp.float32)
    )
    return (
        jnp.einsum("ijd,dc->ijc", scaled, out_weight, preferred_element_type=jnp.float32) * gate
    ).astype(jnp.bfloat16)


def shards(pair_rows, in_gain, left_weight, right_weight, mid_gain, out_weight, out_gate):
    ready, left, right = project_pair(pair_rows, in_gain, left_weight, right_weight)
    count = pair_rows.shape[0] * lax.axis_size("first")
    left_lines, right_lines = (
        lax.all_to_all(left, "first", split_axis=2, concat_axis=0, tiled=True),
        lax.all_to_all(right, "first", split_axis=2, concat_axis=0, tiled=True),
    )
    strip = jnp.einsum(
        "kid,kjd->ijd",
        lax.all_gather(left_lines, "second", axis=1, tiled=True),
        right_lines,
        preferred_element_type=jnp.float32,
    )
    strip = (strip * count ** (-0.5)).astype(jnp.bfloat16)
    mixed = lax.all_to_all(strip, "first", split_axis=0, concat_axis=2, tiled=True)
    return to_pair(mixed, ready, mid_gain, out_weight, out_gate)


def solution(mesh):
    in_specs = (P("first", "second", None), P(), P(), P(), P(), P(), P())
    out_specs = P("first", "second", None)
    return jax.shard_map(shards, mesh=mesh, in_specs=in_specs, out_specs=out_specs, check_vma=False)
```

profile of v0, /device:TPU:1, one launch (start us, length us, event | category | flops | bytes accessed | tf_op | source)
XLA Modules:
  0.0 176.0 jit_solution(14522512396535226179)
XLA Ops:
  6.5 0.0 copy-start
  6.5 0.0 all-gather.2.cloned.1.call-start
  6.5 1.5 convert_reduce_fusion
  8.1 1.8 %fusion.13 = f32[48,48]{1,0:T(8,128)S(1)} fusion(bf16[48,48,128]{2,1,0:T(8,128)(2,1)} %param.7, f32[48,48]{1,0:T(8,128)S(1)} %broadcast_multiply_fusion.1), kind=kLoop, calls=%fused_computation.23 | loop fusion | flops 1177344 | bytes 608256 | tf_op jit(solution)/shard_map/reduce_sum | solution.py:11
  9.9 0.0 copy-done.1
  9.9 1.4 fusion.15
  11.3 0.0 copy-start.2
  11.3 0.8 copy-done.2
  12.1 0.0 copy-done
  12.1 0.3 convolution_convert_fusion
  12.4 1.0 copy.21
  13.4 2.4 %reshape.41 = bf16[16,2,9216]{2,1,0:T(2,128)(2,1)S(1)} reshape(bf16[128,48,48]{2,1,0:T(8,128)(2,1)S(1)} %bitcast.63) | data formatting | bytes 1179648
  15.8 28.7 %all_to_all.45 = bf16[16,2,9216]{2,1,0:T(2,128)(2,1)S(1)} all-to-all(bf16[16,2,9216]{2,1,0:T(2,128)(2,1)S(1)} %reshape.41), channel_id=1, replica_groups=mesh['first'=16,'second'=16] {'first'}, dimensions={0} | all-to-all | bytes 1179648 | tf_op jit(solution)/shard_map/all_to_all | solution.py:39
  44.5 1.5 reshape.42
  46.0 1.4 copy.23
  47.4 0.0 copy-start.3
  47.4 0.0 copy-start.7
  47.4 2.3 %all_to_all.40 = bf16[768,48,8]{0,1,2:T(8,128)(2,1)} reshape(bf16[16,48,48,8]{1,0,2,3:T(8,128)(2,1)S(1)} %copy.23) | data formatting | bytes 1179648 | tf_op jit(solution)/shard_map/all_to_all | solution.py:39
  49.7 0.0 all-gather.2.cloned.1.call-update
  49.7 0.0 copy-done.3
  49.7 0.0 copy-done.7
  49.7 0.3 convolution_convert_fusion.1
  50.0 1.0 copy.18
  51.0 2.4 %reshape.39 = bf16[16,2,9216]{2,1,0:T(2,128)(2,1)S(1)} reshape(bf16[128,48,48]{2,1,0:T(8,128)(2,1)S(1)} %bitcast.64) | data formatting | bytes 1179648
  53.4 21.6 %all_to_all.46 = bf16[16,2,9216]{2,1,0:T(2,128)(2,1)S(1)} all-to-all(bf16[16,2,9216]{2,1,0:T(2,128)(2,1)S(1)} %reshape.39), channel_id=1, replica_groups=mesh['first'=16,'second'=16] {'first'}, dimensions={0} | all-to-all | bytes 1179648 | tf_op jit(solution)/shard_map/all_to_all | solution.py:40
  75.0 1.5 reshape.40
  76.5 1.4 copy.20
  77.9 1.6 all_to_all.36
  79.5 47.3 %all-gather.2.cloned.1.call-done = bf16[768,768,8]{0,1,2:T(8,128)(2,1)} async-done(((bf16[768,48,8]{0,1,2:T(8,128)(2,1)}), bf16[768,768,8]{0,1,2:T(8,128)(2,1)}) %all-gather.2.cloned.1.call-update) | async-done | bytes 9437200 | tf_op jit(solution)/shard_map/all_gather | solution.py:44
  126.8 6.5 %fusion.12 = bf16[768,48,8]{0,1,2:T(8,128)(2,1)S(1)} fusion(bf16[768,48,8]{0,1,2:T(8,128)(2,1)S(1)} %all_to_all.36, bf16[768,768,8]{0,1,2:T(8,128)(2,1)} %all-gather.2.cloned.1.call-done), kind=kOutput, calls=%fused_computation.22 | convolution fusion | flops 453574656 | bytes 10616832 | tf_op jit(solution)/shard_map/kid,kjd->ijd/dot_general | solution.py:42
  133.3 1.1 copy.24
  134.4 0.0 copy-start.4
  134.4 0.0 copy-start.9
  134.4 3.1 %reshape.43 = bf16[16,2,9216]{2,1,0:T(2,128)(2,1)} reshape(bf16[768,8,48]{2,1,0:T(8,128)(2,1)S(1)} %bitcast.65) | data formatting | bytes 1179648
  137.5 7.9 %all-to-all-start.2 = ((bf16[16,2,9216]{2,1,0:T(2,128)(2,1)}), bf16[16,2,9216]{2,1,0:T(2,128)(2,1)S(1)}, u32[]{:S(2)}, u32[]{:S(2)}) async-start(bf16[16,2,9216]{2,1,0:T(2,128)(2,1)} %reshape.43), calls=%async_computation.2 | async-start | bytes 1179648 | tf_op jit(solution)/shard_map/all_to_all | solution.py:49
  145.4 0.0 copy-done.4
  145.4 1.5 fusion.9
  146.9 17.0 %all-to-all-done.2 = bf16[16,2,9216]{2,1,0:T(2,128)(2,1)S(1)} async-done(((bf16[16,2,9216]{2,1,0:T(2,128)(2,1)}), bf16[16,2,9216]{2,1,0:T(2,128)(2,1)S(1)}, u32[]{:S(2)}, u32[]{:S(2)}) %all-to-all-start.2) | async-done | bytes 589856 | tf_op jit(solution)/shard_map/all_to_all | solution.py:49
  163.9 1.5 reshape.44
  165.4 0.0 copy-start.8
  165.5 0.3 bitcast_reduce_fusion
  165.8 0.6 fusion.4
  166.4 0.0 copy-done.8
  166.4 0.0 copy-start.5
  166.5 0.0 copy-start.6
  166.5 0.7 fusion.2
  167.2 0.6 copy-done.5
  167.7 1.4 fusion.10
  (7 shorter events, 0.0 us)
Async XLA Ops:
  6.5 5.6 %copy-start = (bf16[128,128]{1,0:T(8,128)(2,1)S(1)}, bf16[128,128]{1,0:T(8,128)(2,1)}, u32[]{:S(2)}) copy-start(bf16[128,128]{1,0:T(8,128)(2,1)} %param.9) | copy-start | bytes 98308
  6.5 3.3 %copy-start.1 = (bf16[48,48,128]{2,1,0:T(8,128)(2,1)S(1)}, bf16[48,48,128]{2,1,0:T(8,128)(2,1)}, u32[]{:S(2)}) copy-start(bf16[48,48,128]{2,1,0:T(8,128)(2,1)} %param.7) | copy-start | bytes 1769476
  6.5 120.2 %all-gather.2.cloned.1.call-start = ((), (), s32[]{:S(2)}) async-start(), calls=%async_computation.3 | async-start | bytes 10027008 | tf_op jit(solution)/shard_map/all_gather | solution.py:44
  11.3 0.8 copy-start.2
  47.4 2.3 %copy-start.3 = (bf16[48,48,128]{2,1,0:T(8,128)(2,1)S(1)}, bf16[48,48,128]{2,1,0:T(8,128)(2,1)}, u32[]{:S(2)}) copy-start(bf16[48,48,128]{2,1,0:T(8,128)(2,1)} %copy-done.2) | copy-start | bytes 1769476
  47.4 2.3 %copy-start.7 = (bf16[128,128]{1,0:T(8,128)(2,1)S(1)}, bf16[128,128]{1,0:T(8,128)(2,1)}, u32[]{:S(2)}) copy-start(bf16[128,128]{1,0:T(8,128)(2,1)} %param.10) | copy-start | bytes 98308
  134.4 11.0 %copy-start.4 = (bf16[48,48,128]{2,1,0:T(8,128)(2,1)S(1)}, bf16[48,48,128]{2,1,0:T(8,128)(2,1)}, u32[]{:S(2)}) copy-start(bf16[48,48,128]{2,1,0:T(8,128)(2,1)} %copy-done.2) | copy-start | bytes 1769476
  134.4 11.0 %copy-start.9 = (bf16[128,128]{1,0:T(8,128)(2,1)S(1)}, bf16[128,128]{1,0:T(8,128)(2,1)}, u32[]{:S(2)}) copy-start(bf16[128,128]{1,0:T(8,128)(2,1)} %param.13) | copy-start | bytes 98308
  137.5 26.4 %all-to-all-start.2 = ((bf16[16,2,9216]{2,1,0:T(2,128)(2,1)}), bf16[16,2,9216]{2,1,0:T(2,128)(2,1)S(1)}, u32[]{:S(2)}, u32[]{:S(2)}) async-start(bf16[16,2,9216]{2,1,0:T(2,128)(2,1)} %reshape.43), calls=%async_computation.2 | async-start | bytes 1179648 | tf_op jit(solution)/shard_map/all_to_all | solution.py:49
  165.4 1.0 copy-start.8
  166.4 1.3 copy-start.5
  166.5 1.3 copy-start.6
Sparse Core Ops, SparseCore 0:
  49.8 76.8 all-gather.1
where the time goes:
time: 176 us
  waiting for transfers between devices  64.4 us (37%)
  blocking collectives  50.3 us (29%)
  local copies, waits for them, and re-layouts  23.4 us (13%)
  between operations  13.7 us (8%)
  matrix products  9.98 us (6%)
  starting transfers between devices  7.86 us (4%)
  other arithmetic  6.35 us (4%)
    all_gather x1, waiting for transfers between devices, shards(): lax.all_gather(left_lines, 'second', axis=1, tiled=True)  47.3 us
    all_to_all x1, blocking collectives, shards(): lax.all_to_all(left, 'first', split_axis=2, concat_axis=0, tiled=True)  28.7 us
    all_to_all x1, blocking collectives, shards(): lax.all_to_all(right, 'first', split_axis=2, concat_axis=0, tiled=True)  21.6 us
    all_to_all x1, waiting for transfers between devices, shards(): lax.all_to_all(strip, 'first', split_axis=0, concat_axis=2, tiled=True)  17 us
    unnamed x26, local copies, waits for them, and re-layouts  13.9 us
    all_to_all x1, starting transfers between devices, shards(): lax.all_to_all(strip, 'first', split_axis=0, concat_axis=2, tiled=True)  7.86 us
    dot_general x1, matrix products, shards(): jnp.einsum('kid,kjd->ijd', lax.all_gather(left_lines, 'second', axis=1, t...  6.53 us
    all_to_all x2, local copies, waits for them, and re-layouts, shards(): lax.all_to_all(left, 'first', split_axis=2, concat_axis=0, tiled=True)  3.64 us
  transfers between devices with their start and end apart: 2, of which 2 were waited for; matrix products, arithmetic and copies ran while one was open for 5% of the time, Pallas kernels for 0%

commit v1 on v0

v1 whole, which is shorter than its diff:
```python
import functools

import jax
import jax.numpy as jnp
from jax import lax
from jax.experimental import pallas as pl
from jax.experimental.pallas import tpu as pltpu
from jax.sharding import PartitionSpec as P

MESH = pl.DeviceIdType.MESH


def norm_channels(values, channel_gain):
    centred = values - jnp.mean(values, axis=-1, keepdims=True)
    return (
        centred
        * lax.rsqrt(jnp.mean(centred * centred, axis=-1, keepdims=True) + 1e-05)
        * channel_gain
    )


def exchange_kernel(rows, x_ref, o_ref, send_sem, recv_sem, own_sem):
    first, second = lax.axis_index("first"), lax.axis_index("second")
    z, core, y, x = first // 2, first % 2, second // 4, second % 4
    me = z * 16 + second

    def peer(step):
        dz, dy, dx = step // 16, (step // 4) % 4, step % 4
        pz, ps = (z + dz) % 8, ((y + dy) % 4) * 4 + (x + dx) % 4
        return pz * 16 + ps, (pz * 2 + core, ps)

    barrier = pltpu.get_barrier_semaphore()

    def greet(step, _):
        pl.semaphore_signal(barrier, inc=1, device_id=peer(step)[1], device_id_type=MESH)
        return 0

    lax.fori_loop(1, 128, greet, 0)
    pl.semaphore_wait(barrier, 127)

    def send(step, _):
        chip, device = peer(step)
        pltpu.make_async_remote_copy(
            src_ref=x_ref.at[chip],
            dst_ref=o_ref.at[me],
            send_sem=send_sem,
            recv_sem=recv_sem,
            device_id=device,
            device_id_type=MESH,
        ).start()
        return 0

    lax.fori_loop(1, 128, send, 0)
    o_ref[me] = x_ref[me]
    pltpu.make_async_copy(x_ref.at[pl.ds(0, 127)], o_ref.at[pl.ds(0, 127)], recv_sem).wait()
    pltpu.make_async_copy(x_ref.at[pl.ds(0, 127)], o_ref.at[pl.ds(0, 127)], send_sem).wait()


def exchange(x, number):
    return pl.pallas_call(
        functools.partial(exchange_kernel, x.shape[1]),
        out_shape=jax.ShapeDtypeStruct(x.shape, x.dtype),
        in_specs=[pl.BlockSpec(memory_space=pltpu.VMEM)],
        out_specs=pl.BlockSpec(memory_space=pltpu.VMEM),
        scratch_shapes=[pltpu.SemaphoreType.DMA, pltpu.SemaphoreType.DMA, pltpu.SemaphoreType.DMA],
        compiler_params=pltpu.CompilerParams(collective_id=number, has_side_effects=True),
    )(x)


def shards(pair_rows, in_gain, left_weight, right_weight, mid_gain, out_weight, out_gate):
    ready = norm_channels(pair_rows.astype(jnp.float32), in_gain).astype(jnp.bfloat16)
    ready = lax.optimization_barrier(ready)
    both = jnp.concatenate([left_weight, right_weight], axis=1)
    lr = jnp.einsum("kic,cd->dki", ready, both, preferred_element_type=jnp.float32)
    lr = lr.astype(jnp.bfloat16).reshape(2, 128, 18, 128).transpose(1, 0, 2, 3).reshape(128, 36, 128)
    got = exchange(lr, 0).reshape(8, 16, 2, 48, 48)
    got = got.transpose(2, 0, 3, 1, 4).reshape(2, 384, 768)
    part = jnp.einsum("ki,kj->ij", got[0], got[1], preferred_element_type=jnp.float32)
    core = lax.axis_index("first") % 2
    part = part.reshape(8, 2, 48, 768)
    mine = jnp.where(core == 0, part[:, 0], part[:, 1])
    other = jnp.where(core == 0, part[:, 1], part[:, 0])
    swap = [(i, i ^ 1) for i in range(16)]
    mixed = (mine + lax.ppermute(other, "first", swap)) * 768 ** (-0.5)
    mixed = mixed.astype(jnp.bfloat16).reshape(8, 48, 16, 48).transpose(0, 2, 1, 3).reshape(128, 18, 128)
    mixed = exchange(mixed, 1).reshape(128, 48, 48).transpose(1, 2, 0)
    scaled = norm_channels(mixed.astype(jnp.float32), mid_gain).astype(jnp.bfloat16)
    scaled = lax.optimization_barrier(scaled)
    gate = jax.nn.sigmoid(jnp.einsum("ijc,cd->ijd", ready, out_gate, preferred_element_type=jnp.float32))
    return (
        jnp.einsum("ijd,dc->ijc", scaled, out_weight, preferred_element_type=jnp.float32) * gate
    ).astype(jnp.bfloat16)


def solution(mesh):
    in_specs = (P("first", "second", None), P(), P(), P(), P(), P(), P())
    out_specs = P("first", "second", None)
    return jax.shard_map(shards, mesh=mesh, in_specs=in_specs, out_specs=out_specs, check_vma=False)
```

time: 176 us -> 118 us (0.67)
  Pallas kernels: 0 us -> 77.9 us
  waiting for transfers between devices: 64.4 us -> 0.98 us
  blocking collectives: 50.3 us -> 0 us
  between operations: 13.7 us -> 0.3 us
  matrix products: 9.98 us -> 3.83 us
  starting transfers between devices: 7.86 us -> 2.29 us
    pallas_call x0 -> x2, Pallas kernels: none -> 77.9 us  [exchange(): pl.pallas_call(functools.partial(exchange_kernel, x.shape[1]), out_shape=...]
    all_to_all x2 -> x0, blocking collectives: 50.3 us -> none  [the longest x1 28.7 us: shards(): lax.all_to_all(left, 'first', split_axis=2, concat_axis=0, tiled=True)]
    all_gather x1 -> x0, waiting for transfers between devices: 47.3 us -> none  [shards(): lax.all_gather(left_lines, 'second', axis=1, tiled=True)]
    all_to_all x1 -> x0, waiting for transfers between devices: 17 us -> none  [shards(): lax.all_to_all(strip, 'first', split_axis=0, concat_axis=2, tiled=True)]
    reshape x0 -> x7, local copies, waits for them, and re-layouts: none -> 13.8 us  [the longest x3 5.72 us: shards(): mixed.astype(jnp.bfloat16).reshape(8, 48, 16, 48).transpose(0, 2, 1, 3)]
    unnamed x26 -> x24, local copies, waits for them, and re-layouts: 13.9 us -> 1.29 us
    all_to_all x1 -> x0, starting transfers between devices: 7.86 us -> none  [shards(): lax.all_to_all(strip, 'first', split_axis=0, concat_axis=2, tiled=True)]
    all_to_all x4 -> x0, local copies, waits for them, and re-layouts: 6.56 us -> none  [the longest x2 3.64 us: shards(): lax.all_to_all(left, 'first', split_axis=2, concat_axis=0, tiled=True)]
  transfers between devices with their start and end apart: 2 -> 1, of which waited for: 2 -> 1; matrix products, arithmetic and copies ran while one was open for 5% -> 1% of each run, Pallas kernels for 0% -> 0%
where the time goes in v1:
time: 118 us; the launch traced here: 117 us
  Pallas kernels  77.9 us (66%)
  local copies, waits for them, and re-layouts  25.1 us (21%)
  other arithmetic  6.33 us (5%)
  matrix products  3.83 us (3%)
  starting transfers between devices  2.29 us (2%)
    pallas_call x2, Pallas kernels, exchange(): pl.pallas_call(functools.partial(exchange_kernel, x.shape[1]), out_shape=...  77.9 us
    reshape x3, local copies, waits for them, and re-layouts, shards(): mixed.astype(jnp.bfloat16).reshape(8, 48, 16, 48).transpose(0, 2, 1, 3)  5.72 us
    reshape x1, local copies, waits for them, and re-layouts, shards(): got = exchange(lr, 0).reshape(8, 16, 2, 48, 48)  4.35 us
    reshape x3, local copies, waits for them, and re-layouts, shards(): lr.astype(jnp.bfloat16).reshape(2, 128, 18, 128).transpose(1, 0, 2, 3)  3.7 us
    reduce_sum x2, other arithmetic, norm_channels(): jnp.mean(centred * centred, axis=-1, keepdims=True) + 1e-05  2.46 us
  transfers between devices with their start and end apart: 1, of which 1 were waited for; matrix products, arithmetic and copies ran while one was open for 1% of the time, Pallas kernels for 0%

profile of v1, /device:TPU:1, one launch (start us, length us, event | category | flops | bytes accessed | tf_op | source)
XLA Modules:
  0.0 116.7 jit_solution(311988660160857216)
XLA Ops:
  0.0 0.0 copy-start
  0.0 0.0 copy-start.7
  0.0 0.0 copy-start.8
  0.0 1.5 %convert_reduce_fusion = f32[48,48]{1,0:T(8,128)S(1)} fusion(bf16[48,48,128]{2,1,0:T(8,128)(2,1)} %param.7), kind=kLoop, calls=%fused_computation.3 | loop fusion | flops 587520 | bytes 599040 | tf_op jit(solution)/shard_map/reduce_sum | solution.py:14
  1.6 1.8 %fusion.6 = f32[48,48]{1,0:T(8,128)S(1)} fusion(bf16[48,48,128]{2,1,0:T(8,128)(2,1)} %param.7, f32[48,48]{1,0:T(8,128)S(1)} %broadcast_multiply_fusion.1), kind=kLoop, calls=%fused_computation.12 | loop fusion | flops 1177344 | bytes 608256 | tf_op jit(solution)/shard_map/reduce_sum | solution.py:17
  3.3 0.0 copy-done.2
  3.4 0.0 copy-done.10
  3.4 0.8 fusion.8
  4.2 0.0 copy-start.3
  4.2 0.8 copy-done.3
  5.0 0.0 copy-done.7
  5.0 0.0 copy-done.8
  5.0 0.4 convolution_convert_fusion
  5.4 0.3 reshape.55
  5.8 1.5 %copy.27 = bf16[2,128,18,128]{3,1,2,0:T(8,128)(2,1)S(1)} copy(bf16[2,128,18,128]{1,0,3,2:T(2,128)(2,1)S(1)} %reshape.55) | data formatting | bytes 2359296 | tf_op jit(solution)/shard_map/reshape | solution.py:75
  7.3 1.8 %copy.28.x_ref = bf16[128,36,128]{2,1,0:T(8,128)(2,1)} copy(bf16[128,36,128]{2,0,1:T(8,128)(2,1)S(1)} %bitcast.67) | data formatting | bytes 2359296 | tf_op jit(solution)/shard_map/reshape | solution.py:75
  9.1 47.9 %shard_map.73 = bf16[128,36,128]{2,1,0:T(8,128)(2,1)} custom-call(bf16[128,36,128]{2,1,0:T(8,128)(2,1)} %copy.28.x_ref), custom_call_target="tpu_custom_call" | custom-call | tf_op jit(solution)/shard_map/pallas_call | solution.py:60
  57.0 4.3 %reshape.57 = bf16[8,16,2,48,48]{4,3,2,1,0:T(8,128)(2,1)S(1)} reshape(bf16[128,36,128]{2,1,0:T(8,128)(2,1)} %shard_map.73) | data formatting | bytes 2359296 | tf_op jit(solution)/shard_map/reshape | solution.py:76
  61.4 1.7 %fusion.20 = (bf16[1,8,48,16,48]{4,2,0,3,1:T(8,128)(2,1)}, bf16[1,8,48,16,48]{4,2,0,3,1:T(8,128)(2,1)S(1)}) fusion(bf16[2,8,48,16,48]{4,2,0,3,1:T(8,128)(2,1)S(1)} %bitcast.65), kind=kLoop, calls=%fused_computation.35 | loop fusion | bytes 2359296 | tf_op jit(solution)/shard_map/slice | solution.py:78
  63.1 0.4 copy.29
  63.5 0.0 copy-start.1
  63.5 2.3 %squeeze.4 = bf16[384,768]{1,0:T(8,128)(2,1)} reshape(bf16[1,8,48,16,48]{4,3,2,1,0:T(8,128)(2,1)S(1)} %copy.29) | data formatting | bytes 1179648 | tf_op jit(solution)/shard_map/squeeze | solution.py:78
  65.8 2.1 %copy.30 = bf16[768,384]{1,0:T(8,128)(2,1)} copy(bf16[768,384]{0,1:T(8,128)(2,1)} %bitcast.69) | data formatting | bytes 1179648 | tf_op jit(solution)/shard_map/ki,kj->ij/dot_general | solution.py:78
  67.9 0.0 copy-done.1
  67.9 0.4 copy.31
  68.3 0.0 copy-start.5
  68.4 1.6 %reshape.62 = bf16[384,768,1,1]{1,0,2,3:T(8,128)(2,1)S(1)} reshape(bf16[1,8,48,16,48]{4,3,2,1,0:T(8,128)(2,1)S(1)} %copy.31) | data formatting | bytes 1179648 | tf_op jit(solution)/shard_map/squeeze | solution.py:78
  69.9 0.8 fusion.13
  70.7 0.0 copy-start.4
  70.7 0.1 select_bitcast_fusion
  70.9 2.3 %collective-permute-start = (f32[8,48,768]{2,1,0:T(8,128)S(1)}, f32[8,48,768]{2,1,0:T(8,128)S(1)}, u32[]{:S(2)}, u32[]{:S(2)}) collective-permute-start(f32[8,48,768]{2,1,0:T(8,128)S(1)} %select_bitcast_fusion), channel_id=1, source_target_pairs={{0,16},{16,0},{32,48},{48,32},{64,80},{80,64},{96,112},{112,96},{1... | collective-permute-start | bytes 3538952 | tf_op jit(solution)/shard_map/ppermute | solution.py:84
  73.2 0.0 copy-done.4
  73.2 1.5 %fusion.4 = f32[48,48,128]{2,1,0:T(8,128)} fusion(bf16[48,48,128]{2,1,0:T(8,128)(2,1)S(1)} %copy-done.4, bf16[128,128]{1,0:T(8,128)(2,1)S(1)} %copy-done), kind=kOutput, calls=%fused_computation.10 | convolution fusion | flops 76382208 | bytes 1802240 | tf_op jit(solution)/shard_map/ijc,cd->ijd/dot_general | solution.py:89
  74.6 1.0 collective-permute-done
  75.6 0.3 fusion.12
  75.9 1.9 %reshape.58 = bf16[8,48,16,48]{3,2,1,0:T(8,128)(2,1)S(1)} reshape(bf16[8,48,768]{2,1,0:T(8,128)(2,1)S(1)} %fusion.12) | data formatting | bytes 1179648 | tf_op jit(solution)/shard_map/reshape | solution.py:85
  77.8 0.4 copy.41
  78.3 3.4 %reshape.59.x_ref = bf16[128,18,128]{2,1,0:T(8,128)(2,1)} reshape(bf16[8,16,48,48]{3,2,1,0:T(8,128)(2,1)S(1)} %bitcast.66) | data formatting | bytes 1179648 | tf_op jit(solution)/shard_map/reshape | solution.py:85
  81.6 30.0 %shard_map.74 = bf16[128,18,128]{2,1,0:T(8,128)(2,1)} custom-call(bf16[128,18,128]{2,1,0:T(8,128)(2,1)} %reshape.59.x_ref), custom_call_target="tpu_custom_call" | custom-call | tf_op jit(solution)/shard_map/pallas_call | solution.py:60
  111.7 1.5 %copy.37 = f32[128,18,128]{0,2,1:T(8,128)S(1)} copy(bf16[128,18,128]{2,1,0:T(8,128)(2,1)} %shard_map.74) | data formatting | bytes 1769472 | tf_op jit(solution)/shard_map/convert_element_type | solution.py:87
  113.2 0.0 copy-start.11
  113.2 0.4 reduce_sum.38
  113.6 0.7 multiply_reduce_fusion
  114.3 0.0 copy-start.6
  114.3 0.0 copy-start.9
  114.4 0.8 multiply_convert_fusion
  115.2 0.4 copy-done.6
  115.6 1.1 fusion.5
  (10 shorter events, 0.0 us)
Async XLA Ops:
  0.0 73.2 %copy-start = (bf16[128,128]{1,0:T(8,128)(2,1)S(1)}, bf16[128,128]{1,0:T(8,128)(2,1)}, u32[]{:S(2)}) copy-start(bf16[128,128]{1,0:T(8,128)(2,1)} %param.13) | copy-start | bytes 98308
  0.0 3.3 %copy-start.2 = (bf16[48,48,128]{2,1,0:T(8,128)(2,1)S(1)}, bf16[48,48,128]{2,1,0:T(8,128)(2,1)}, u32[]{:S(2)}) copy-start(bf16[48,48,128]{2,1,0:T(8,128)(2,1)} %param.7) | copy-start | bytes 1769476
  0.0 3.4 %copy-start.10 = (f32[128]{0:T(128)S(1)}, f32[128]{0:T(128)}, u32[]{:S(2)}) copy-start(f32[128]{0:T(128)} %param.8) | copy-start | bytes 1540
  0.0 4.9 %copy-start.7 = (bf16[128,128]{1,0:T(8,128)(2,1)S(1)}, bf16[128,128]{1,0:T(8,128)(2,1)}, u32[]{:S(2)}) copy-start(bf16[128,128]{1,0:T(8,128)(2,1)} %param.10) | copy-start | bytes 98308
  0.0 4.9 %copy-start.8 = (bf16[128,128]{1,0:T(8,128)(2,1)S(1)}, bf16[128,128]{1,0:T(8,128)(2,1)}, u32[]{:S(2)}) copy-start(bf16[128,128]{1,0:T(8,128)(2,1)} %param.9) | copy-start | bytes 98308
  4.2 0.8 copy-start.3
  63.5 4.4 %copy-start.1 = (bf16[1,8,48,16,48]{4,2,0,3,1:T(8,128)(2,1)S(1)}, bf16[1,8,48,16,48]{4,2,0,3,1:T(8,128)(2,1)}, u32[]{:S(2)}) copy-start(bf16[1,8,48,16,48]{4,2,0,3,1:T(8,128)(2,1)} %get-tuple-element.5) | copy-start | bytes 1769476
  68.3 1.6 %copy-start.5 = (bf16[768,384]{1,0:T(8,128)(2,1)S(1)}, bf16[768,384]{1,0:T(8,128)(2,1)}, u32[]{:S(2)}) copy-start(bf16[768,384]{1,0:T(8,128)(2,1)} %copy.30) | copy-start | bytes 1769476
  70.7 2.5 %copy-start.4 = (bf16[48,48,128]{2,1,0:T(8,128)(2,1)S(1)}, bf16[48,48,128]{2,1,0:T(8,128)(2,1)}, u32[]{:S(2)}) copy-start(bf16[48,48,128]{2,1,0:T(8,128)(2,1)} %copy-done.3) | copy-start | bytes 1769476
  70.9 4.8 %collective-permute-start = (f32[8,48,768]{2,1,0:T(8,128)S(1)}, f32[8,48,768]{2,1,0:T(8,128)S(1)}, u32[]{:S(2)}, u32[]{:S(2)}) collective-permute-start(f32[8,48,768]{2,1,0:T(8,128)S(1)} %select_bitcast_fusion), channel_id=1, source_target_pairs={{0,16},{16,0},{32,48},{48,32},{64,80},{80,64},{96,112},{112,96},{1... | collective-permute-start | bytes 3538952 | tf_op jit(solution)/shard_map/ppermute | solution.py:84
  113.2 1.1 copy-start.11
  114.3 1.3 %copy-start.6 = (f32[48,48,128]{2,1,0:T(8,128)S(1)}, f32[48,48,128]{2,1,0:T(8,128)}, u32[]{:S(2)}) copy-start(f32[48,48,128]{2,1,0:T(8,128)} %fusion.4) | copy-start | bytes 3538948
  114.3 1.3 %copy-start.9 = (bf16[128,128]{1,0:T(8,128)(2,1)S(1)}, bf16[128,128]{1,0:T(8,128)(2,1)}, u32[]{:S(2)}) copy-start(bf16[128,128]{1,0:T(8,128)(2,1)} %param.12) | copy-start | bytes 98308

commit v2 on v1

v2 whole, which is shorter than its diff:
```python
import jax
import jax.numpy as jnp
from jax import lax
from jax.experimental import pallas as pl
from jax.experimental.pallas import tpu as pltpu
from jax.sharding import PartitionSpec as P

MESH = pl.DeviceIdType.MESH
F32, BF16 = jnp.float32, jnp.bfloat16
PITCH = 104
HALF = 56


def swap_blocks(parts):
    block = lax.broadcasted_iota(jnp.int32, parts[0].shape, 1) // 16
    for h in (4, 2, 1):
        low = (block // h) % 2 == 0
        out = list(parts)
        for p in range(8):
            if p // h % 2 == 0:
                a, b = parts[p], parts[p + h]
                out[p] = jnp.where(low, a, pltpu.roll(b, 16 * h, 1))
                out[p + h] = jnp.where(low, pltpu.roll(a, 128 - 16 * h, 1), b)
        parts = out
    return parts


def kernel(
    x_ref, in_gain, left_w, right_w, mid_gain, out_w, gate_w, o_ref,
    weights, ready, wide, sent, got, spread, left, right, sums, other, wide2, sent2, got2, spread2, gates, gain_col,
    send_a, recv_a, send_b, recv_b, send_c, recv_c,
):
    first, second = lax.axis_index("first"), lax.axis_index("second")
    z, core, y, x = first // 2, first % 2, second // 4, second % 4
    me = second * 8 + z
    partner = (z * 2 + 1 - core, second)

    def peer(step):
        dz, dy, dx = step // 16, (step // 4) % 4, step % 4
        pz, ps = (z + dz) % 8, ((y + dy) % 4) * 4 + (x + dx) % 4
        return ps * 8 + pz, (pz * 2 + core, ps)

    barrier = pltpu.get_barrier_semaphore()

    def greet(step, _):
        pl.semaphore_signal(barrier, inc=1, device_id=peer(step)[1], device_id_type=MESH)
        return 0

    lax.fori_loop(1, 128, greet, 0)
    pl.semaphore_signal(barrier, inc=1, device_id=partner, device_id_type=MESH)

    weights[0:128, :] = left_w[...].T
    weights[128:256, :] = right_w[...].T
    gain_col[...] = jnp.broadcast_to(mid_gain[...], (128, 128)).T

    def project(r, _):
        ao, bc = r // 3, r % 3
        v = x_ref[pl.ds(ao * 8, 8), pl.ds(pl.multiple_of(bc * 16, 16), 16), :].astype(F32).reshape(128, 128)
        v = v - jnp.mean(v, axis=1, keepdims=True)
        v = v * lax.rsqrt(jnp.mean(v * v, axis=1, keepdims=True) + 1e-05) * in_gain[...]
        v = v.astype(BF16)
        ready[r] = v
        both = lax.dot_general(weights[...], v, (((1,), (1,)), ((), ())), preferred_element_type=F32)
        wide[pl.ds(r, 128, stride=36), :] = both[0:128]
        wide[pl.ds(18 + r, 128, stride=36), :] = both[128:256]
        return 0

    lax.fori_loop(0, 18, project, 0)

    def pack(i, _):
        rows = pl.ds(pl.multiple_of(i * 128, 128), 128)
        sent[rows, :] = wide[rows, :].astype(BF16)
        return 0

    lax.fori_loop(0, 36, pack, 0)
    pl.semaphore_wait(barrier, 128)

    def send(step, _):
        chip, device = peer(step)
        pltpu.make_async_remote_copy(
            src_ref=sent.at[pl.ds(chip * 36, 36)],
            dst_ref=got.at[pl.ds(me * 36, 36)],
            send_sem=send_a,
            recv_sem=recv_a,
            device_id=device,
            device_id_type=MESH,
        ).start()
        return 0

    lax.fori_loop(1, 128, send, 0)

    def gate(r, _):
        g = jnp.dot(ready[r], gate_w[...], preferred_element_type=F32)
        gates[r] = jax.nn.sigmoid(g)
        return 0

    lax.fori_loop(0, 18, gate, 0)
    all_a = pl.ds(0, 127 * 36)
    pltpu.make_async_copy(sent.at[all_a], got.at[all_a], recv_a).wait()

    def unpack(i, _):
        rows = pl.ds(pl.multiple_of(i * 128, 128), 128)
        spread[rows, :] = got[rows, :].astype(F32)
        return 0

    lax.fori_loop(0, 36, unpack, 0)
    own = wide[pl.ds(me * 36, 36), :]
    spread[pl.ds(me * 36, 36), :] = own.astype(BF16).astype(F32)

    def gather(g, _):
        lanes = pl.ds(pl.multiple_of(g * 128, 128), 128)
        for side in range(2):
            pieces = []
            for ao in range(6):
                parts = []
                for p in range(8):
                    q = g * 8 + p
                    start = (q // 3) * 288 + q % 3 + side * 18 + ao * 3
                    parts.append(spread[pl.ds(start, 8, stride=36), :])
                parts = swap_blocks(parts)
                rows = jnp.concatenate(parts, axis=0).astype(BF16)
                if side == 1:
                    right[ao * 64 : ao * 64 + 64, lanes] = rows
                else:
                    pieces.append(rows)
                    if ao % 2 == 1:
                        block = jnp.concatenate(pieces, axis=0)
                        left[lanes, (ao // 2) * 128 : (ao // 2) * 128 + 128] = block.T
                        pieces = []
        return 0

    lax.fori_loop(0, 6, gather, 0)

    def multiply(t, _):
        rows = pl.ds(pl.multiple_of(t * 192, 64), 192)
        part = jnp.dot(left[rows, :], right[...], preferred_element_type=F32)
        for u in range(2):
            at = (t * 2 + u) * PITCH
            for g in range(6):
                sums[g, pl.ds(pl.multiple_of(at, 8), 96), :] = part[u * 96 : u * 96 + 96, g * 128 : g * 128 + 128]
        for u in range(2):
            zz = t * 2 + u
            pltpu.make_async_remote_copy(
                src_ref=sums.at[:, pl.ds(pl.multiple_of(zz * PITCH + (1 - core) * 48, 8), 48), :],
                dst_ref=other.at[:, pl.ds(pl.multiple_of(zz * HALF, 8), 48), :],
                send_sem=send_b.at[zz],
                recv_sem=recv_b.at[zz],
                device_id=partner,
                device_id_type=MESH,
            ).start()
        return 0

    lax.fori_loop(0, 4, multiply, 0)
    for i in range(8):
        pltpu.make_async_copy(
            sums.at[:, pl.ds(0, 48), :], other.at[:, pl.ds(0, 48), :], recv_b.at[i]
        ).wait()

    def scatter(g, _):
        for ao in range(6):
            parts = []
            for a8 in range(8):
                i = ao * 8 + a8
                mine = sums[g, pl.ds(core * 48 + i, 8, stride=PITCH), :]
                theirs = other[g, pl.ds(i, 8, stride=HALF), :]
                parts.append((mine + theirs) * 768 ** (-0.5))
            parts = swap_blocks(parts)
            for p in range(8):
                q = g * 8 + p
                start = (q // 3) * 144 + q % 3 + ao * 3
                wide2[pl.ds(start, 8, stride=18), :] = parts[p]
        return 0

    lax.fori_loop(0, 6, scatter, 0)

    def pack2(i, _):
        rows = pl.ds(pl.multiple_of(i * 128, 128), 128)
        sent2[rows, :] = wide2[rows, :].astype(BF16)
        return 0

    lax.fori_loop(0, 18, pack2, 0)

    def send2(step, _):
        chip, device = peer(step)
        pltpu.make_async_remote_copy(
            src_ref=sent2.at[pl.ds(chip * 18, 18)],
            dst_ref=got2.at[pl.ds(me * 18, 18)],
            send_sem=send_c,
            recv_sem=recv_c,
            device_id=device,
            device_id_type=MESH,
        ).start()
        return 0

    lax.fori_loop(1, 128, send2, 0)
    all_c = pl.ds(0, 127 * 18)
    pltpu.make_async_copy(sent2.at[all_c], got2.at[all_c], recv_c).wait()

    def unpack2(i, _):
        rows = pl.ds(pl.multiple_of(i * 128, 128), 128)
        spread2[rows, :] = got2[rows, :].astype(F32)
        return 0

    lax.fori_loop(0, 18, unpack2, 0)
    own2 = wide2[pl.ds(me * 18, 18), :]
    spread2[pl.ds(me * 18, 18), :] = own2.astype(BF16).astype(F32)

    def finish(r, _):
        ao, bc = r // 3, r % 3
        v = spread2[pl.ds(r, 128, stride=18), :]
        v = v - jnp.mean(v, axis=0, keepdims=True)
        v = v * lax.rsqrt(jnp.mean(v * v, axis=0, keepdims=True) + 1e-05) * gain_col[...]
        out = jnp.dot(v.astype(BF16).T, out_w[...], preferred_element_type=F32) * gates[r]
        o_ref[pl.ds(ao * 8, 8), pl.ds(pl.multiple_of(bc * 16, 16), 16), :] = out.astype(BF16).reshape(8, 16, 128)
        return 0

    lax.fori_loop(0, 18, finish, 0)
    pltpu.make_async_copy(sent.at[all_a], got.at[all_a], send_a).wait()
    for i in range(8):
        pltpu.make_async_copy(
            sums.at[:, pl.ds(0, 48), :], other.at[:, pl.ds(0, 48), :], send_b.at[i]
        ).wait()
    pltpu.make_async_copy(sent2.at[all_c], got2.at[all_c], send_c).wait()


def shards(pair_rows, in_gain, left_weight, right_weight, mid_gain, out_weight, out_gate):
    vmem = pl.BlockSpec(memory_space=pltpu.VMEM)
    return pl.pallas_call(
        kernel,
        out_shape=jax.ShapeDtypeStruct(pair_rows.shape, BF16),
        in_specs=[vmem] * 7,
        out_specs=vmem,
        scratch_shapes=[
            pltpu.VMEM((256, 128), BF16),
            pltpu.VMEM((18, 128, 128), BF16),
            pltpu.VMEM((128 * 36, 128), F32),
            pltpu.VMEM((128 * 36, 128), BF16),
            pltpu.VMEM((128 * 36, 128), BF16),
            pltpu.VMEM((128 * 36, 128), F32),
            pltpu.VMEM((768, 384), BF16),
            pltpu.VMEM((384, 768), BF16),
            pltpu.VMEM((6, 8 * PITCH, 128), F32),
            pltpu.VMEM((6, 8 * HALF, 128), F32),
            pltpu.VMEM((128 * 18, 128), F32),
            pltpu.VMEM((128 * 18, 128), BF16),
            pltpu.VMEM((128 * 18, 128), BF16),
            pltpu.VMEM((128 * 18, 128), F32),
            pltpu.VMEM((18, 128, 128), F32),
            pltpu.VMEM((128, 128), F32),
        ]
        + [pltpu.SemaphoreType.DMA] * 2
        + [pltpu.SemaphoreType.DMA((8,))] * 2
        + [pltpu.SemaphoreType.DMA] * 2,
        compiler_params=pltpu.CompilerParams(collective_id=0, has_side_effects=True),
    )(
        pair_rows, in_gain.reshape(1, 128), left_weight, right_weight,
        mid_gain.reshape(1, 128), out_weight, out_gate,
    )


def solution(mesh):
    in_specs = (P("first", "second", None), P(), P(), P(), P(), P(), P())
    out_specs = P("first", "second", None)
    return jax.shard_map(shards, mesh=mesh, in_specs=in_specs, out_specs=out_specs, check_vma=False)
```

time: 118 us -> 83 us (0.70)
  local copies, waits for them, and re-layouts: 25.1 us -> 1.92 us
  other arithmetic: 6.33 us -> 0 us
  matrix products: 3.83 us -> 0 us
  Pallas kernels: 77.9 us -> 80.2 us
  starting transfers between devices: 2.29 us -> 0 us
    reshape x7 -> x0, local copies, waits for them, and re-layouts: 13.8 us -> none  [the longest x3 5.72 us: shards(): mixed.astype(jnp.bfloat16).reshape(8, 48, 16, 48).transpose(0, 2, 1, 3)]
    reduce_sum x4 -> x0, other arithmetic: 4.33 us -> none  [the longest x2 2.46 us: norm_channels(): jnp.mean(centred * centred, axis=-1, keepdims=True) + 1e-05]
    squeeze x2 -> x0, local copies, waits for them, and re-layouts: 3.84 us -> none  [the longest x1 2.27 us: shards(): got[0]]
    dot_general x4 -> x0, matrix products: 3.83 us -> none  [the longest x1 1.49 us: shards(): jnp.einsum('ijc,cd->ijd', ready, out_gate, preferred_element_type=jnp.flo...]
    slice x3 -> x0, local copies, waits for them, and re-layouts: 2.53 us -> none  [the longest x2 2.12 us: shards(): got[1]]
    pallas_call x2 -> x1, Pallas kernels: 77.9 us -> 80.2 us  [shards(): pl.pallas_call(kernel, out_shape=jax.ShapeDtypeStruct(pair_rows.shape, BF...]
    ppermute x1 -> x0, starting transfers between devices: 2.29 us -> none  [shards(): mixed = (mine + lax.ppermute(other, 'first', swap)) * 768 ** (-0.5)]
    dot_general x1 -> x0, local copies, waits for them, and re-layouts: 2.14 us -> none  [shards(): jnp.einsum('ki,kj->ij', got[0], got[1], preferred_element_type=jnp.float32)]
  transfers between devices with their start and end apart: 1 -> 0, of which waited for: 1 -> 0; matrix products, arithmetic and copies ran while one was open for 1% -> 0% of each run, Pallas kernels for 0% -> 0%
where the time goes in v2:
time: 83 us; the launch traced here: 82.1 us
  Pallas kernels  80.2 us (97%)
  local copies, waits for them, and re-layouts  1.92 us (2%)
    pallas_call x1, Pallas kernels, shards(): pl.pallas_call(kernel, out_shape=jax.ShapeDtypeStruct(pair_rows.shape, BF...  80.2 us
    unnamed x1, local copies, waits for them, and re-layouts  1.92 us

profile of v2, /device:TPU:1, one launch (start us, length us, event | category | flops | bytes accessed | tf_op | source)
XLA Modules:
  0.0 82.1 jit_solution(11142149636370370799)
XLA Ops:
  0.0 80.2 %shard_map.73 = bf16[48,48,128]{2,1,0:T(8,128)(2,1)} custom-call(bf16[48,48,128]{2,1,0:T(8,128)(2,1)} %x_ref.1, f32[1,128]{1,0:T(1,128)} %bitcast.2, bf16[128,128]{1,0:T(8,128)(2,1)} %left_w.1, bf16[128,128]{1,0:T(8,128)(2,1)} %right_w.1, f32[1,128]{1,0:T(1,128)} %bitcast.3, bf16[128,128]{1,0:T(8,128)(2,1)} %out_w.1, bf16[128,128]{1,0:T(8,128)(2,1)} %gate_w.1), custom_call_target="tpu_custom_call" | custom-call | tf_op jit(solution)/shard_map/pallas_call | solution.py:228
  80.2 1.9 %copy.9 = bf16[48,48,128]{2,1,0:T(8,128)(2,1)} copy(bf16[48,48,128]{2,1,0:T(8,128)(2,1)} %shard_map.73) | data formatting | bytes 1179648

commit v3 on v2

v3 whole, which is shorter than its diff:
```python
import jax
import jax.numpy as jnp
from jax import lax
from jax.experimental import pallas as pl
from jax.experimental.pallas import tpu as pltpu
from jax.sharding import PartitionSpec as P

MESH = pl.DeviceIdType.MESH
F32, BF16 = jnp.float32, jnp.bfloat16
PITCH = 24


def swap_blocks(parts):
    block = lax.broadcasted_iota(jnp.int32, parts[0].shape, 1) // 16
    for h in (4, 2, 1):
        low = (block // h) % 2 == 0
        out = list(parts)
        for p in range(8):
            if p // h % 2 == 0:
                a, b = parts[p], parts[p + h]
                out[p] = jnp.where(low, a, pltpu.roll(b, 16 * h, 1))
                out[p + h] = jnp.where(low, pltpu.roll(a, 128 - 16 * h, 1), b)
        parts = out
    return parts


def kernel(
    x_ref, in_gain, left_w, right_w, mid_gain, out_w, gate_w, o_ref,
    weights, ready, wide, sent, got, spread, left, right, sums, outgoing, other, wide2, sent2, got2, spread2, gates, gain_col,
    send_a, recv_a, send_b, recv_b, send_c, recv_c,
):
    first, second = lax.axis_index("first"), lax.axis_index("second")
    z, core, y, x = lax.div(first, 2), lax.rem(first, 2), lax.div(second, 4), lax.rem(second, 4)
    me = second * 8 + z
    partner = (first + 1 - 2 * core, second)
    columns = [lax.rem(x + dx, 4) for dx in (1, 2, 3, 0)]

    def each_peer(act):
        for dz in (4, 3, 5, 2, 6, 1, 7, 0):
            pz = lax.rem(z + dz, 8)

            def line(dy, _, pz=pz, count=4):
                row = lax.rem(y + dy, 4) * 4
                for column in columns[:count]:
                    ps = row + column
                    act(ps * 8 + pz, (pz * 2 + core, ps))
                return 0

            lax.fori_loop(1, 4, line, 0)
            line(0, 0, count=4 if dz else 3)

    barrier = pltpu.get_barrier_semaphore()
    each_peer(lambda chip, device: pl.semaphore_signal(barrier, inc=1, device_id=device, device_id_type=MESH))
    pl.semaphore_signal(barrier, inc=1, device_id=partner, device_id_type=MESH)

    weights[0] = left_w[...].T
    weights[1] = right_w[...].T
    gain_col[...] = jnp.broadcast_to(mid_gain[...], (128, 128)).T

    def turn(side, r, v):
        rows = lax.dot_general(weights[side], v, (((1,), (1,)), ((), ())), preferred_element_type=F32)
        wide[side, pl.ds(r, 128, stride=18), :] = rows

    def norm(r, _):
        ao, bc = lax.div(r, 3), lax.rem(r, 3)
        v = x_ref[pl.ds(ao * 8, 8), pl.ds(pl.multiple_of(bc * 16, 16), 16), :].astype(F32).reshape(128, 128)
        v = v - jnp.mean(v, axis=1, keepdims=True)
        v = v * lax.rsqrt(jnp.mean(v * v, axis=1, keepdims=True) + 1e-05) * in_gain[...]
        v = v.astype(BF16)
        ready[r] = v
        turn(1, r, v)
        return 0

    def project(r, _):
        turn(0, r, ready[r])
        return 0

    def pack(side):
        def step(i, _):
            rows = pl.ds(pl.multiple_of(i * 256, 256), 256)
            sent[side, rows, :] = wide[side, rows, :].astype(BF16)
            return 0

        lax.fori_loop(0, 9, step, 0)

    def send(side):
        def start(chip, device):
            pltpu.make_async_remote_copy(
                src_ref=sent.at[side, pl.ds(chip * 18, 18)],
                dst_ref=got.at[side, pl.ds(me * 18, 18)],
                send_sem=send_a.at[side],
                recv_sem=recv_a.at[side],
                device_id=device,
                device_id_type=MESH,
            ).start()

        each_peer(start)

    lax.fori_loop(0, 18, norm, 0, unroll=3)
    pack(1)
    pl.semaphore_wait(barrier, 128)
    send(1)
    lax.fori_loop(0, 18, project, 0, unroll=3)
    pack(0)
    send(0)

    def gate(r, _):
        g = jnp.dot(ready[r], gate_w[...], preferred_element_type=F32)
        gates[r] = jax.nn.sigmoid(g)
        return 0

    lax.fori_loop(0, 18, gate, 0, unroll=3)
    most = pl.ds(0, 127 * 18)

    def unpack(side):
        def step(i, _):
            rows = pl.ds(pl.multiple_of(i * 256, 256), 256)
            spread[side, rows, :] = got[side, rows, :].astype(F32)
            return 0

        lax.fori_loop(0, 9, step, 0)
        own = wide[side, pl.ds(me * 18, 18), :]
        spread[side, pl.ds(me * 18, 18), :] = own.astype(BF16).astype(F32)

    def gather_right(t, _):
        bc, h = lax.div(t, 2), lax.rem(t, 2)
        lanes = pl.ds(pl.multiple_of(t * 128, 128), 128)
        for ao in range(6):
            parts = [spread[1, pl.ds((h * 8 + p) * 144 + ao * 3 + bc, 8, stride=18), :] for p in range(8)]
            right[ao * 64 : ao * 64 + 64, lanes] = jnp.concatenate(swap_blocks(parts), axis=0).astype(BF16)
        return 0

    def gather_left(t, _):
        bc, h = lax.div(t, 2), lax.rem(t, 2)
        for pair in range(3):
            pieces = []
            for ao in (2 * pair, 2 * pair + 1):
                parts = [
                    spread[0, pl.ds((h * 8 + p % 4 * 2 + p // 4) * 144 + ao * 3 + bc, 8, stride=18), :]
                    for p in range(8)
                ]
                pieces += swap_blocks(parts)
            block = jnp.concatenate(pieces, axis=0).astype(BF16).T
            lanes = slice(pair * 128, pair * 128 + 128)
            left[pl.ds(pl.multiple_of((1 - core) * 384 + t * 64, 64), 64), lanes] = block[0:64]
            left[pl.ds(pl.multiple_of(core * 384 + t * 64, 64), 64), lanes] = block[64:128]
        return 0

    pltpu.make_async_copy(sent.at[1, most], got.at[1, most], recv_a.at[1]).wait()
    unpack(1)
    lax.fori_loop(0, 6, gather_right, 0)
    pltpu.make_async_copy(sent.at[0, most], got.at[0, most], recv_a.at[0]).wait()
    unpack(0)
    lax.fori_loop(0, 6, gather_left, 0)

    def product(target, half, bc):
        rows = pl.ds(pl.multiple_of(half * 384 + bc * 128, 128), 128)
        part = jnp.dot(left[rows, :], right[...], preferred_element_type=F32)
        for zz in range(8):
            for g in range(6):
                target[g, pl.ds(pl.multiple_of((bc * 8 + zz) * PITCH, 8), 16), :] = part[
                    zz * 16 : zz * 16 + 16, g * 128 : g * 128 + 128
                ]

    def multiply(bc, _):
        product(outgoing, 0, bc)
        for zz in range(8):
            rows = pl.ds(pl.multiple_of((bc * 8 + zz) * PITCH, 8), 16)
            pltpu.make_async_remote_copy(
                src_ref=outgoing.at[:, rows, :],
                dst_ref=other.at[:, rows, :],
                send_sem=send_b.at[bc],
                recv_sem=recv_b.at[bc],
                device_id=partner,
                device_id_type=MESH,
            ).start()
        return 0

    def multiply_own(bc, _):
        product(sums, 1, bc)
        return 0

    lax.fori_loop(0, 3, multiply, 0)
    lax.fori_loop(0, 3, multiply_own, 0)
    third = pl.ds(0, 128)

    def scatter(bc):
        def step(g, _):
            h, bd = lax.rem(g, 2), lax.div(g, 2)
            for ao in (2 * bc, 2 * bc + 1):
                parts = []
                for a8 in range(8):
                    rows = pl.ds(bc * 8 * PITCH + ao % 2 * 8 + a8, 8, stride=PITCH)
                    parts.append((sums[g, rows, :] + other[g, rows, :]) * 768 ** (-0.5))
                for p, part in enumerate(swap_blocks(parts)):
                    wide2[pl.ds((h * 8 + p) * 144 + ao * 3 + bd, 8, stride=18), :] = part
            return 0

        lax.fori_loop(0, 6, step, 0)

    for bc in range(3):
        pltpu.make_async_copy(outgoing.at[:, third, :], other.at[:, third, :], recv_b.at[bc]).wait()
        scatter(bc)

    def pack2(i, _):
        rows = pl.ds(pl.multiple_of(i * 256, 256), 256)
        sent2[rows, :] = wide2[rows, :].astype(BF16)
        return 0

    lax.fori_loop(0, 9, pack2, 0)

    def start2(chip, device):
        pltpu.make_async_remote_copy(
            src_ref=sent2.at[pl.ds(chip * 18, 18)],
            dst_ref=got2.at[pl.ds(me * 18, 18)],
            send_sem=send_c,
            recv_sem=recv_c,
            device_id=device,
            device_id_type=MESH,
        ).start()

    each_peer(start2)
    pltpu.make_async_copy(sent2.at[most], got2.at[most], recv_c).wait()

    def unpack2(i, _):
        rows = pl.ds(pl.multiple_of(i * 256, 256), 256)
        spread2[rows, :] = got2[rows, :].astype(F32)
        return 0

    lax.fori_loop(0, 9, unpack2, 0)
    own2 = wide2[pl.ds(me * 18, 18), :]
    spread2[pl.ds(me * 18, 18), :] = own2.astype(BF16).astype(F32)

    def finish(r, _):
        ao, bc = lax.div(r, 3), lax.rem(r, 3)
        v = spread2[pl.ds(r, 128, stride=18), :]
        v = v - jnp.mean(v, axis=0, keepdims=True)
        v = v * lax.rsqrt(jnp.mean(v * v, axis=0, keepdims=True) + 1e-05) * gain_col[...]
        out = jnp.dot(v.astype(BF16).T, out_w[...], preferred_element_type=F32) * gates[r]
        o_ref[pl.ds(ao * 8, 8), pl.ds(pl.multiple_of(bc * 16, 16), 16), :] = out.astype(BF16).reshape(8, 16, 128)
        return 0

    lax.fori_loop(0, 18, finish, 0, unroll=3)
    for side in range(2):
        pltpu.make_async_copy(sent.at[side, most], got.at[side, most], send_a.at[side]).wait()
    for bc in range(3):
        pltpu.make_async_copy(outgoing.at[:, third, :], other.at[:, third, :], send_b.at[bc]).wait()
    pltpu.make_async_copy(sent2.at[most], got2.at[most], send_c).wait()


def shards(pair_rows, in_gain, left_weight, right_weight, mid_gain, out_weight, out_gate):
    vmem = pl.BlockSpec(memory_space=pltpu.VMEM)
    return pl.pallas_call(
        kernel,
        out_shape=jax.ShapeDtypeStruct(pair_rows.shape, BF16),
        in_specs=[vmem] * 7,
        out_specs=vmem,
        scratch_shapes=[
            pltpu.VMEM((2, 128, 128), BF16),
            pltpu.VMEM((18, 128, 128), BF16),
            pltpu.VMEM((2, 128 * 18, 128), F32),
            pltpu.VMEM((2, 128 * 18, 128), BF16),
            pltpu.VMEM((2, 128 * 18, 128), BF16),
            pltpu.VMEM((2, 128 * 18, 128), F32),
            pltpu.VMEM((768, 384), BF16),
            pltpu.VMEM((384, 768), BF16),
            pltpu.VMEM((6, 24 * PITCH, 128), F32),
            pltpu.VMEM((6, 24 * PITCH, 128), F32),
            pltpu.VMEM((6, 24 * PITCH, 128), F32),
            pltpu.VMEM((128 * 18, 128), F32),
            pltpu.VMEM((128 * 18, 128), BF16),
            pltpu.VMEM((128 * 18, 128), BF16),
            pltpu.VMEM((128 * 18, 128), F32),
            pltpu.VMEM((18, 128, 128), F32),
            pltpu.VMEM((128, 128), F32),
            pltpu.SemaphoreType.DMA((2,)),
            pltpu.SemaphoreType.DMA((2,)),
            pltpu.SemaphoreType.DMA((3,)),
            pltpu.SemaphoreType.DMA((3,)),
            pltpu.SemaphoreType.DMA,
            pltpu.SemaphoreType.DMA,
        ],
        compiler_params=pltpu.CompilerParams(collective_id=0, has_side_effects=True),
    )(
        pair_rows, in_gain.reshape(1, 128), left_weight, right_weight,
        mid_gain.reshape(1, 128), out_weight, out_gate,
    )


def solution(mesh):
    in_specs = (P("first", "second", None), P(), P(), P(), P(), P(), P())
    out_specs = P("first", "second", None)
    return jax.shard_map(shards, mesh=mesh, in_specs=in_specs, out_specs=out_specs, check_vma=False)
```

time: 83 us -> 72.2 us (0.87)
  Pallas kernels: 80.2 us -> 70.1 us
    pallas_call x1, Pallas kernels: 80.2 us -> 70.1 us  [shards(): pl.pallas_call(kernel, out_shape=jax.ShapeDtypeStruct(pair_rows.shape, BF...]
where the time goes in v3:
time: 72.2 us; the launch traced here: 72.1 us
  Pallas kernels  70.1 us (97%)
  local copies, waits for them, and re-layouts  1.92 us (3%)
    pallas_call x1, Pallas kernels, shards(): pl.pallas_call(kernel, out_shape=jax.ShapeDtypeStruct(pair_rows.shape, BF...  70.1 us
    unnamed x1, local copies, waits for them, and re-layouts  1.92 us

profile of v3, /device:TPU:1, one launch (start us, length us, event | category | flops | bytes accessed | tf_op | source)
XLA Modules:
  0.0 72.1 jit_solution(5556349749415580118)
XLA Ops:
  0.0 70.1 %shard_map.73 = bf16[48,48,128]{2,1,0:T(8,128)(2,1)} custom-call(bf16[48,48,128]{2,1,0:T(8,128)(2,1)} %x_ref.1, f32[1,128]{1,0:T(1,128)} %bitcast.2, bf16[128,128]{1,0:T(8,128)(2,1)} %left_w.1, bf16[128,128]{1,0:T(8,128)(2,1)} %right_w.1, f32[1,128]{1,0:T(1,128)} %bitcast.3, bf16[128,128]{1,0:T(8,128)(2,1)} %out_w.1, bf16[128,128]{1,0:T(8,128)(2,1)} %gate_w.1), custom_call_target="tpu_custom_call" | custom-call | tf_op jit(solution)/shard_map/pallas_call | solution.py:253
  70.1 1.9 %copy.9 = bf16[48,48,128]{2,1,0:T(8,128)(2,1)} copy(bf16[48,48,128]{2,1,0:T(8,128)(2,1)} %shard_map.73) | data formatting | bytes 1179648

commit v4 on v3

v4 whole, which is shorter than its diff:
```python
import jax
import jax.numpy as jnp
from jax import lax
from jax.experimental import pallas as pl
from jax.experimental.pallas import tpu as pltpu
from jax.sharding import PartitionSpec as P

MESH = pl.DeviceIdType.MESH
F32, BF16 = jnp.float32, jnp.bfloat16
PITCH = 24


def swap_blocks(parts):
    block = lax.broadcasted_iota(jnp.int32, parts[0].shape, 1) // 16
    for h in (4, 2, 1):
        low = (block // h) % 2 == 0
        out = list(parts)
        for p in range(8):
            if p // h % 2 == 0:
                a, b = parts[p], parts[p + h]
                out[p] = jnp.where(low, a, pltpu.roll(b, 16 * h, 1))
                out[p + h] = jnp.where(low, pltpu.roll(a, 128 - 16 * h, 1), b)
        parts = out
    return parts


def kernel(
    x_hbm, in_gain_hbm, left_hbm, right_hbm, mid_gain_hbm, out_hbm, gate_hbm, o_ref,
    x_ref, in_gain, left_w, right_w, mid_gain, out_w, gate_w,
    weights, ready, wide_r, wide_a, wide_b, sent_r, sent_a, sent_b, got_r, got_a, got_b,
    spread_r, spread_a, spread_b, left, right, sums, outgoing, other,
    wide2_a, wide2_b, sent2_a, sent2_b, got2_a, got2_b, spread2_a, spread2_b, gates, gain_col,
    load_sem, send_in, recv_in, send_swap, recv_swap, send_out, recv_out,
):
    first, second = lax.axis_index("first"), lax.axis_index("second")
    z, core, y, x = lax.div(first, 2), lax.rem(first, 2), lax.div(second, 4), lax.rem(second, 4)
    me = second * 8 + z
    partner = (first + 1 - 2 * core, second)
    columns = [lax.rem(x + dx, 4) for dx in (1, 2, 3, 0)]

    loads = [
        pltpu.make_async_copy(src, dst, load_sem.at[i])
        for i, (src, dst) in enumerate(
            [
                (x_hbm, x_ref), (right_hbm, right_w), (in_gain_hbm, in_gain), (left_hbm, left_w),
                (mid_gain_hbm, mid_gain), (out_hbm, out_w), (gate_hbm, gate_w),
            ]
        )
    ]
    for load in loads:
        load.start()

    def each_peer(act):
        for dz in (4, 3, 5, 2, 6, 1, 7, 0):
            pz = lax.rem(z + dz, 8)

            def line(dy, _, pz=pz, count=4):
                row = lax.rem(y + dy, 4) * 4
                for column in columns[:count]:
                    ps = row + column
                    act(ps * 8 + pz, (pz * 2 + core, ps))
                return 0

            lax.fori_loop(1, 4, line, 0)
            line(0, 0, count=4 if dz else 3)

    barrier = pltpu.get_barrier_semaphore()
    each_peer(lambda chip, device: pl.semaphore_signal(barrier, inc=1, device_id=device, device_id_type=MESH))
    pl.semaphore_signal(barrier, inc=1, device_id=partner, device_id_type=MESH)
    for load in loads:
        load.wait()

    weights[0] = left_w[...].T
    weights[1] = right_w[...].T
    gain_col[...] = jnp.broadcast_to(mid_gain[...], (128, 128)).T

    def turn(side, v):
        return lax.dot_general(weights[side], v, (((1,), (1,)), ((), ())), preferred_element_type=F32)

    def norm(r, _):
        ao, bc = lax.div(r, 3), lax.rem(r, 3)
        v = x_ref[pl.ds(ao * 8, 8), pl.ds(pl.multiple_of(bc * 16, 16), 16), :].astype(F32).reshape(128, 128)
        v = v - jnp.mean(v, axis=1, keepdims=True)
        v = v * lax.rsqrt(jnp.mean(v * v, axis=1, keepdims=True) + 1e-05) * in_gain[...]
        v = v.astype(BF16)
        ready[r] = v
        wide_r[pl.ds(r, 128, stride=18), :] = turn(1, v)
        return 0

    def project(ao, _):
        for bc in range(3):
            rows = turn(0, ready[ao * 3 + bc])
            if bc < 2:
                wide_a[pl.ds(bc * 6 + ao, 128, stride=12), :] = rows
            else:
                wide_b[pl.ds(ao, 128, stride=6), :] = rows
        return 0

    def convert(source, target):
        def step(i, _):
            rows = pl.ds(pl.multiple_of(i * 256, 256), 256)
            target[rows, :] = source[rows, :].astype(target.dtype)
            return 0

        lax.fori_loop(0, source.shape[0] // 256, step, 0)

    def send(source, target, send_sem, recv_sem):
        rows = source.shape[0] // 128

        def start(chip, device):
            pltpu.make_async_remote_copy(
                src_ref=source.at[pl.ds(chip * rows, rows)],
                dst_ref=target.at[pl.ds(me * rows, rows)],
                send_sem=send_sem,
                recv_sem=recv_sem,
                device_id=device,
                device_id_type=MESH,
            ).start()

        each_peer(start)

    def settle(source, target, sem):
        rows = pl.ds(0, source.shape[0] // 128 * 127)
        pltpu.make_async_copy(source.at[rows], target.at[rows], sem).wait()

    def receive(wide, source, target, spread, sem):
        settle(source, target, sem)
        convert(target, spread)
        rows = source.shape[0] // 128
        own = wide[pl.ds(me * rows, rows), :]
        spread[pl.ds(me * rows, rows), :] = own.astype(BF16).astype(F32)

    lax.fori_loop(0, 18, norm, 0, unroll=3)
    convert(wide_r, sent_r)
    pl.semaphore_wait(barrier, 128)
    send(sent_r, got_r, send_in.at[0], recv_in.at[0])
    lax.fori_loop(0, 6, project, 0)
    convert(wide_a, sent_a)
    send(sent_a, got_a, send_in.at[1], recv_in.at[1])
    convert(wide_b, sent_b)
    send(sent_b, got_b, send_in.at[2], recv_in.at[2])

    def gate(r, _):
        g = jnp.dot(ready[r], gate_w[...], preferred_element_type=F32)
        gates[r] = jax.nn.sigmoid(g)
        return 0

    lax.fori_loop(0, 18, gate, 0, unroll=3)

    def gather_right(t, _):
        bc, h = lax.div(t, 2), lax.rem(t, 2)
        lanes = pl.ds(pl.multiple_of(t * 128, 128), 128)
        for ao in range(6):
            parts = [spread_r[pl.ds((h * 8 + p) * 144 + ao * 3 + bc, 8, stride=18), :] for p in range(8)]
            right[ao * 64 : ao * 64 + 64, lanes] = jnp.concatenate(swap_blocks(parts), axis=0).astype(BF16)
        return 0

    def gather_left(spread, t, at):
        rows = spread.shape[0] // 128
        for pair in range(3):
            pieces = []
            for ao in (2 * pair, 2 * pair + 1):
                pieces += swap_blocks(
                    [
                        spread[pl.ds(at + (p % 4 * 2 + p // 4) * 8 * rows + ao, 8, stride=rows), :]
                        for p in range(8)
                    ]
                )
            block = jnp.concatenate(pieces, axis=0).astype(BF16).T
            lanes = slice(pair * 128, pair * 128 + 128)
            left[pl.ds(pl.multiple_of((1 - core) * 384 + t * 64, 64), 64), lanes] = block[0:64]
            left[pl.ds(pl.multiple_of(core * 384 + t * 64, 64), 64), lanes] = block[64:128]

    def gather_a(t, _):
        gather_left(spread_a, t, lax.rem(t, 2) * 768 + lax.div(t, 2) * 6)
        return 0

    def gather_b(h, _):
        gather_left(spread_b, 4 + h, h * 384)
        return 0

    def product(target, half, bc):
        rows = pl.ds(pl.multiple_of(half * 384 + bc * 128, 128), 128)
        part = jnp.dot(left[rows, :], right[...], preferred_element_type=F32)
        for zz in range(8):
            for g in range(6):
                target[g, pl.ds(pl.multiple_of((bc * 8 + zz) * PITCH, 8), 16), :] = part[
                    zz * 16 : zz * 16 + 16, g * 128 : g * 128 + 128
                ]

    def multiply(bc, _):
        product(outgoing, 0, bc)
        for zz in range(8):
            rows = pl.ds(pl.multiple_of((bc * 8 + zz) * PITCH, 8), 16)
            pltpu.make_async_remote_copy(
                src_ref=outgoing.at[:, rows, :],
                dst_ref=other.at[:, rows, :],
                send_sem=send_swap.at[bc],
                recv_sem=recv_swap.at[bc],
                device_id=partner,
                device_id_type=MESH,
            ).start()
        return 0

    def multiply_own(bc, _):
        product(sums, 1, bc)
        return 0

    third = pl.ds(0, 128)

    def scatter(wide, bc, skip):
        pltpu.make_async_copy(outgoing.at[:, third, :], other.at[:, third, :], recv_swap.at[bc]).wait()
        count = wide.shape[0] // 128

        def step(g, _):
            h, bd = lax.rem(g, 2), lax.div(g, 2)
            for ao in (2 * bc, 2 * bc + 1):
                parts = []
                for a8 in range(8):
                    rows = pl.ds(bc * 8 * PITCH + ao % 2 * 8 + a8, 8, stride=PITCH)
                    parts.append((sums[g, rows, :] + other[g, rows, :]) * 768 ** (-0.5))
                for p, part in enumerate(swap_blocks(parts)):
                    wide[pl.ds((h * 8 + p) * 8 * count + (ao - skip) * 3 + bd, 8, stride=count), :] = part
            return 0

        lax.fori_loop(0, 6, step, 0, unroll=2)

    def finish(spread, skip):
        def step(r, _):
            v = spread[pl.ds(r, 128, stride=spread.shape[0] // 128), :]
            v = v - jnp.mean(v, axis=0, keepdims=True)
            v = v * lax.rsqrt(jnp.mean(v * v, axis=0, keepdims=True) + 1e-05) * gain_col[...]
            out = jnp.dot(v.astype(BF16).T, out_w[...], preferred_element_type=F32) * gates[skip * 3 + r]
            ao, bc = skip + lax.div(r, 3), lax.rem(r, 3)
            o_ref[pl.ds(ao * 8, 8), pl.ds(pl.multiple_of(bc * 16, 16), 16), :] = out.astype(BF16).reshape(8, 16, 128)
            return 0

        lax.fori_loop(0, spread.shape[0] // 128, step, 0, unroll=3)

    receive(wide_r, sent_r, got_r, spread_r, recv_in.at[0])
    lax.fori_loop(0, 6, gather_right, 0)
    receive(wide_a, sent_a, got_a, spread_a, recv_in.at[1])
    lax.fori_loop(0, 4, gather_a, 0)
    lax.fori_loop(0, 2, multiply, 0)
    lax.fori_loop(0, 2, multiply_own, 0)
    scatter(wide2_a, 0, 0)
    scatter(wide2_a, 1, 0)
    convert(wide2_a, sent2_a)
    send(sent2_a, got2_a, send_out.at[0], recv_out.at[0])
    receive(wide_b, sent_b, got_b, spread_b, recv_in.at[2])
    lax.fori_loop(0, 2, gather_b, 0)
    multiply(2, 0)
    multiply_own(2, 0)
    scatter(wide2_b, 2, 4)
    convert(wide2_b, sent2_b)
    send(sent2_b, got2_b, send_out.at[1], recv_out.at[1])
    receive(wide2_a, sent2_a, got2_a, spread2_a, recv_out.at[0])
    finish(spread2_a, 0)
    receive(wide2_b, sent2_b, got2_b, spread2_b, recv_out.at[1])
    finish(spread2_b, 4)

    settle(sent_r, got_r, send_in.at[0])
    settle(sent_a, got_a, send_in.at[1])
    settle(sent_b, got_b, send_in.at[2])
    settle(sent2_a, got2_a, send_out.at[0])
    settle(sent2_b, got2_b, send_out.at[1])
    for bc in range(3):
        pltpu.make_async_copy(outgoing.at[:, third, :], other.at[:, third, :], send_swap.at[bc]).wait()


def shards(pair_rows, in_gain, left_weight, right_weight, mid_gain, out_weight, out_gate):
    hbm = pl.BlockSpec(memory_space=pltpu.HBM)
    square = pltpu.VMEM((128, 128), BF16)
    line = pltpu.VMEM((1, 128), F32)
    flat = [18, 12, 6]
    return pl.pallas_call(
        kernel,
        out_shape=pltpu.VMEM(pair_rows.shape, BF16),
        in_specs=[hbm] * 7,
        out_specs=pl.BlockSpec(memory_space=pltpu.VMEM),
        scratch_shapes=[
            pltpu.VMEM(pair_rows.shape, BF16), line, square, square, line, square, square,
            pltpu.VMEM((2, 128, 128), BF16),
            pltpu.VMEM((18, 128, 128), BF16),
        ]
        + [pltpu.VMEM((128 * n, 128), F32) for n in flat]
        + [pltpu.VMEM((128 * n, 128), BF16) for n in flat]
        + [pltpu.VMEM((128 * n, 128), BF16) for n in flat]
        + [pltpu.VMEM((128 * n, 128), F32) for n in flat]
        + [
            pltpu.VMEM((768, 384), BF16),
            pltpu.VMEM((384, 768), BF16),
            pltpu.VMEM((6, 24 * PITCH, 128), F32),
            pltpu.VMEM((6, 24 * PITCH, 128), F32),
            pltpu.VMEM((6, 24 * PITCH, 128), F32),
        ]
        + [pltpu.VMEM((128 * n, 128), F32) for n in flat[1:]]
        + [pltpu.VMEM((128 * n, 128), BF16) for n in flat[1:]]
        + [pltpu.VMEM((128 * n, 128), BF16) for n in flat[1:]]
        + [pltpu.VMEM((128 * n, 128), F32) for n in flat[1:]]
        + [
            pltpu.VMEM((18, 128, 128), F32),
            pltpu.VMEM((128, 128), F32),
        ]
        + [pltpu.SemaphoreType.DMA((n,)) for n in (7, 3, 3, 3, 3, 2, 2)],
        compiler_params=pltpu.CompilerParams(
            collective_id=0, has_side_effects=True
        ),
    )(
        pair_rows, in_gain.reshape(1, 128), left_weight, right_weight,
        mid_gain.reshape(1, 128), out_weight, out_gate,
    )


def solution(mesh):
    in_specs = (P("first", "second", None), P(), P(), P(), P(), P(), P())
    out_specs = P("first", "second", None)
    return jax.shard_map(shards, mesh=mesh, in_specs=in_specs, out_specs=out_specs, check_vma=False)
```

time: 72.2 us -> 62.3 us (0.86)
  Pallas kernels: 70.1 us -> 61.4 us
  local copies, waits for them, and re-layouts: 1.92 us -> 0.82 us
    pallas_call x1, Pallas kernels: 70.1 us -> 61.4 us  [shards(): pl.pallas_call(kernel, out_shape=pltpu.VMEM(pair_rows.shape, BF16), in_sp...]
    unnamed x1, local copies, waits for them, and re-layouts: 1.92 us -> 0.82 us
where the time goes in v4:
time: 62.3 us
  Pallas kernels  61.4 us (99%)
  local copies, waits for them, and re-layouts  0.82 us (1%)
    pallas_call x1, Pallas kernels, shards(): pl.pallas_call(kernel, out_shape=pltpu.VMEM(pair_rows.shape, BF16), in_sp...  61.4 us

profile of v4, /device:TPU:1, one launch (start us, length us, event | category | flops | bytes accessed | tf_op | source)
XLA Modules:
  0.0 62.3 jit_solution(8408785661639559564)
XLA Ops:
  0.0 61.4 %shard_map.73 = bf16[48,48,128]{2,1,0:T(8,128)(2,1)S(1)} custom-call(bf16[48,48,128]{2,1,0:T(8,128)(2,1)} %x_hbm.1, f32[1,128]{1,0:T(1,128)} %bitcast.2, bf16[128,128]{1,0:T(8,128)(2,1)} %left_hbm.1, bf16[128,128]{1,0:T(8,128)(2,1)} %right_hbm.1, f32[1,128]{1,0:T(1,128)} %bitcast.3, bf16[128,128]{1,0:T(8,128)(2,1)} %out_hbm.1, bf16[128,128]{1,0:T(8,128)(2,1)} %gate_hbm.1), custom_call_target="tpu_custom_call" | custom-call | tf_op jit(solution)/shard_map/pallas_call | solution.py:276
  61.5 0.8 %copy.9 = bf16[48,48,128]{2,1,0:T(8,128)(2,1)} copy(bf16[48,48,128]{2,1,0:T(8,128)(2,1)S(1)} %shard_map.73) | data formatting | bytes 1179648

commit v5 on v4

v5 whole, which is shorter than its diff:
```python
import jax
import jax.numpy as jnp
from jax import lax
from jax.experimental import pallas as pl
from jax.experimental.pallas import tpu as pltpu
from jax.sharding import PartitionSpec as P

MESH = pl.DeviceIdType.MESH
F32, BF16 = jnp.float32, jnp.bfloat16
PITCH = 24


def swap_blocks(parts):
    block = lax.broadcasted_iota(jnp.int32, parts[0].shape, 1) // 16
    for h in (4, 2, 1):
        low = (block // h) % 2 == 0
        out = list(parts)
        for p in range(8):
            if p // h % 2 == 0:
                a, b = parts[p], parts[p + h]
                out[p] = jnp.where(low, a, pltpu.roll(b, 16 * h, 1))
                out[p + h] = jnp.where(low, pltpu.roll(a, 128 - 16 * h, 1), b)
        parts = out
    return parts


def kernel(
    x_hbm, in_gain_hbm, left_hbm, right_hbm, mid_gain_hbm, out_hbm, gate_hbm, o_ref,
    x_ref, in_gain, left_w, right_w, mid_gain, out_w, gate_w,
    weights, ready, wide_r, sent_r, got_r, spread_r, wide_l, sent_l, got_l, spread_l,
    left, right, sums, outgoing, other, wide_o, sent_o, got_o, spread_o, gates, gain_col,
    load_sem, send_in, recv_in, send_swap, recv_swap, send_out, recv_out,
):
    first, second = lax.axis_index("first"), lax.axis_index("second")
    z, core, y, x = lax.div(first, 2), lax.rem(first, 2), lax.div(second, 4), lax.rem(second, 4)
    me = second * 8 + z
    partner = (first + 1 - 2 * core, second)
    layers = [lax.rem(z + dz, 8) for dz in (0, 4, 1, 7, 2, 6, 3, 5)]

    loads = [
        pltpu.make_async_copy(src, dst, load_sem.at[i])
        for i, (src, dst) in enumerate(
            [
                (x_hbm, x_ref), (right_hbm, right_w), (in_gain_hbm, in_gain), (left_hbm, left_w),
                (mid_gain_hbm, mid_gain), (out_hbm, out_w), (gate_hbm, gate_w),
            ]
        )
    ]
    for load in loads:
        load.start()

    def each_peer(act):
        def ahead(i):
            return jnp.where(i == 0, 2, jnp.where(i == 1, 1, jnp.where(i == 2, 3, 0)))

        def column(e, _):
            ps = lax.rem(y + ahead(lax.div(e, 4)), 4) * 4 + lax.rem(x + ahead(lax.rem(e, 4)), 4)
            for pz in layers:
                act(ps * 8 + pz, (pz * 2 + core, ps))
            return 0

        lax.fori_loop(0, 15, column, 0)
        for pz in layers[1:]:
            act(second * 8 + pz, (pz * 2 + core, second))

    barrier = pltpu.get_barrier_semaphore()
    each_peer(lambda chip, device: pl.semaphore_signal(barrier, inc=1, device_id=device, device_id_type=MESH))
    pl.semaphore_signal(barrier, inc=1, device_id=partner, device_id_type=MESH)
    for load in loads:
        load.wait()

    weights[0] = left_w[...].T
    weights[1] = right_w[...].T
    gain_col[...] = jnp.broadcast_to(mid_gain[...], (128, 128)).T

    def turn(side, v):
        return lax.dot_general(weights[side], v, (((1,), (1,)), ((), ())), preferred_element_type=F32)

    def norm(r, _):
        ao, bc = lax.div(r, 3), lax.rem(r, 3)
        v = x_ref[pl.ds(ao * 8, 8), pl.ds(pl.multiple_of(bc * 16, 16), 16), :].astype(F32).reshape(128, 128)
        v = v - jnp.mean(v, axis=1, keepdims=True)
        v = v * lax.rsqrt(jnp.mean(v * v, axis=1, keepdims=True) + 1e-05) * in_gain[...]
        v = v.astype(BF16)
        ready[r] = v
        wide_r[pl.ds(r, 128, stride=18), :] = turn(1, v)
        return 0

    def project(ao, _):
        for bc in range(3):
            wide_l[bc, pl.ds(ao, 128, stride=6), :] = turn(0, ready[ao * 3 + bc])
        return 0

    def convert(source, target):
        def step(i, _):
            rows = pl.ds(pl.multiple_of(i * 256, 256), 256)
            target[rows, :] = source[rows, :].astype(target.dtype)
            return 0

        lax.fori_loop(0, source.shape[0] // 256, step, 0)

    def send(source, target, send_sem, recv_sem):
        rows = source.shape[0] // 128

        def start(chip, device):
            pltpu.make_async_remote_copy(
                src_ref=source.at[pl.ds(chip * rows, rows)],
                dst_ref=target.at[pl.ds(me * rows, rows)],
                send_sem=send_sem,
                recv_sem=recv_sem,
                device_id=device,
                device_id_type=MESH,
            ).start()

        each_peer(start)

    def settle(source, target, sem):
        rows = pl.ds(0, source.shape[0] // 128 * 127)
        pltpu.make_async_copy(source.at[rows], target.at[rows], sem).wait()

    def receive(wide, source, target, spread, sem):
        settle(source, target, sem)
        convert(target, spread)
        rows = source.shape[0] // 128
        own = wide[pl.ds(me * rows, rows), :]
        spread[pl.ds(me * rows, rows), :] = own.astype(BF16).astype(F32)

    lax.fori_loop(0, 18, norm, 0, unroll=3)
    convert(wide_r, sent_r)
    pl.semaphore_wait(barrier, 128)
    send(sent_r, got_r, send_in.at[0], recv_in.at[0])
    lax.fori_loop(0, 6, project, 0)

    def send_left(bc):
        convert(wide_l.at[bc], sent_l.at[bc])
        send(sent_l.at[bc], got_l.at[bc], send_in.at[1 + bc], recv_in.at[1 + bc])

    send_left(0)
    send_left(1)

    def gate(r, _):
        g = jnp.dot(ready[r], gate_w[...], preferred_element_type=F32)
        gates[r] = jax.nn.sigmoid(g)
        return 0

    lax.fori_loop(0, 18, gate, 0, unroll=3)

    def gather_right(t, _):
        bc, h = lax.div(t, 2), lax.rem(t, 2)
        lanes = pl.ds(pl.multiple_of(t * 128, 128), 128)
        for ao in range(6):
            parts = [spread_r[pl.ds((h * 8 + p) * 144 + ao * 3 + bc, 8, stride=18), :] for p in range(8)]
            right[ao * 64 : ao * 64 + 64, lanes] = jnp.concatenate(swap_blocks(parts), axis=0).astype(BF16)
        return 0

    def gather_left(t, _):
        bc, h = lax.div(t, 2), lax.rem(t, 2)
        for pair in range(3):
            pieces = []
            for ao in (2 * pair, 2 * pair + 1):
                pieces += swap_blocks(
                    [
                        spread_l[bc, pl.ds((h * 8 + p % 4 * 2 + p // 4) * 48 + ao, 8, stride=6), :]
                        for p in range(8)
                    ]
                )
            block = jnp.concatenate(pieces, axis=0).astype(BF16).T
            lanes = slice(pair * 128, pair * 128 + 128)
            left[pl.ds(pl.multiple_of((1 - core) * 384 + t * 64, 64), 64), lanes] = block[0:64]
            left[pl.ds(pl.multiple_of(core * 384 + t * 64, 64), 64), lanes] = block[64:128]
        return 0

    def product(target, half, bc):
        rows = pl.ds(pl.multiple_of(half * 384 + bc * 128, 128), 128)
        part = jnp.dot(left[rows, :], right[...], preferred_element_type=F32)
        for zz in range(8):
            for g in range(6):
                target[g, pl.ds(pl.multiple_of((bc * 8 + zz) * PITCH, 8), 16), :] = part[
                    zz * 16 : zz * 16 + 16, g * 128 : g * 128 + 128
                ]

    def multiply(bc):
        product(outgoing, 0, bc)
        for zz in range(8):
            rows = pl.ds((bc * 8 + zz) * PITCH, 16)
            pltpu.make_async_remote_copy(
                src_ref=outgoing.at[:, rows, :],
                dst_ref=other.at[:, rows, :],
                send_sem=send_swap.at[bc],
                recv_sem=recv_swap.at[bc],
                device_id=partner,
                device_id_type=MESH,
            ).start()
        product(sums, 1, bc)

    third = pl.ds(0, 128)

    def scatter(bc):
        pltpu.make_async_copy(outgoing.at[:, third, :], other.at[:, third, :], recv_swap.at[bc]).wait()

        def add(g, _):
            for zz in range(8):
                rows = pl.ds((bc * 8 + zz) * PITCH, 16)
                sums[g, rows, :] = (sums[g, rows, :] + other[g, rows, :]) * 768 ** (-0.5)
            return 0

        lax.fori_loop(0, 6, add, 0, unroll=2)

        def step(g, _):
            h, bd = lax.rem(g, 2), lax.div(g, 2)
            for ao in range(2):
                parts = [
                    sums[g, pl.ds(bc * 8 * PITCH + ao * 8 + a8, 8, stride=PITCH), :] for a8 in range(8)
                ]
                for p, part in enumerate(swap_blocks(parts)):
                    wide_o[bc, pl.ds((h * 8 + p) * 48 + ao * 3 + bd, 8, stride=6), :] = part
            return 0

        lax.fori_loop(0, 6, step, 0, unroll=3)

    def finish(part):
        def step(r, _):
            v = spread_o[part, pl.ds(r, 128, stride=6), :]
            v = v - jnp.mean(v, axis=0, keepdims=True)
            v = v * lax.rsqrt(jnp.mean(v * v, axis=0, keepdims=True) + 1e-05) * gain_col[...]
            out = jnp.dot(v.astype(BF16).T, out_w[...], preferred_element_type=F32) * gates[part * 6 + r]
            ao, bc = part * 2 + lax.div(r, 3), lax.rem(r, 3)
            o_ref[pl.ds(ao * 8, 8), pl.ds(pl.multiple_of(bc * 16, 16), 16), :] = out.astype(BF16).reshape(8, 16, 128)
            return 0

        lax.fori_loop(0, 6, step, 0, unroll=3)

    receive(wide_r, sent_r, got_r, spread_r, recv_in.at[0])
    send_left(2)
    lax.fori_loop(0, 6, gather_right, 0, unroll=2)
    for bc in range(3):
        receive(wide_l.at[bc], sent_l.at[bc], got_l.at[bc], spread_l.at[bc], recv_in.at[1 + bc])
        lax.fori_loop(2 * bc, 2 * bc + 2, gather_left, 0, unroll=2)
        multiply(bc)
        scatter(bc)
        convert(wide_o.at[bc], sent_o.at[bc])
        send(sent_o.at[bc], got_o.at[bc], send_out.at[bc], recv_out.at[bc])
    for part in range(3):
        receive(wide_o.at[part], sent_o.at[part], got_o.at[part], spread_o.at[part], recv_out.at[part])
        finish(part)

    settle(sent_r, got_r, send_in.at[0])
    for part in range(3):
        settle(sent_l.at[part], got_l.at[part], send_in.at[1 + part])
        settle(sent_o.at[part], got_o.at[part], send_out.at[part])
        pltpu.make_async_copy(outgoing.at[:, third, :], other.at[:, third, :], send_swap.at[part]).wait()


def shards(pair_rows, in_gain, left_weight, right_weight, mid_gain, out_weight, out_gate):
    hbm = pl.BlockSpec(memory_space=pltpu.HBM)
    square = pltpu.VMEM((128, 128), BF16)
    line = pltpu.VMEM((1, 128), F32)
    def flat(*parts):
        return [pltpu.VMEM(parts + (128,), dtype) for dtype in (F32, BF16, BF16, F32)]

    return pl.pallas_call(
        kernel,
        out_shape=pltpu.VMEM(pair_rows.shape, BF16),
        in_specs=[hbm] * 7,
        out_specs=pl.BlockSpec(memory_space=pltpu.VMEM),
        scratch_shapes=[
            pltpu.VMEM(pair_rows.shape, BF16), line, square, square, line, square, square,
            pltpu.VMEM((2, 128, 128), BF16),
            pltpu.VMEM((18, 128, 128), BF16),
        ]
        + flat(128 * 18)
        + flat(3, 128 * 6)
        + [
            pltpu.VMEM((768, 384), BF16),
            pltpu.VMEM((384, 768), BF16),
            pltpu.VMEM((6, 24 * PITCH, 128), F32),
            pltpu.VMEM((6, 24 * PITCH, 128), F32),
            pltpu.VMEM((6, 24 * PITCH, 128), F32),
        ]
        + flat(3, 128 * 6)
        + [
            pltpu.VMEM((18, 128, 128), F32),
            pltpu.VMEM((128, 128), F32),
        ]
        + [pltpu.SemaphoreType.DMA((n,)) for n in (7, 4, 4, 3, 3, 3, 3)],
        compiler_params=pltpu.CompilerParams(
            collective_id=0, has_side_effects=True
        ),
    )(
        pair_rows, in_gain.reshape(1, 128), left_weight, right_weight,
        mid_gain.reshape(1, 128), out_weight, out_gate,
    )


def solution(mesh):
    in_specs = (P("first", "second", None), P(), P(), P(), P(), P(), P())
    out_specs = P("first", "second", None)
    return jax.shard_map(shards, mesh=mesh, in_specs=in_specs, out_specs=out_specs, check_vma=False)
```

time: 62.3 us -> 56.9 us (0.913)
  Pallas kernels: 61.4 us -> 56 us
    pallas_call x1, Pallas kernels: 61.4 us -> 56 us  [shards(): pl.pallas_call(kernel, out_shape=pltpu.VMEM(pair_rows.shape, BF16), in_sp...]
where the time goes in v5:
time: 56.9 us; the launch traced here: 56.8 us
  Pallas kernels  56 us (98%)
  local copies, waits for them, and re-layouts  0.82 us (1%)
    pallas_call x1, Pallas kernels, shards(): pl.pallas_call(kernel, out_shape=pltpu.VMEM(pair_rows.shape, BF16), in_sp...  56 us

profile of v5, /device:TPU:1, one launch (start us, length us, event | category | flops | bytes accessed | tf_op | source)
XLA Modules:
  0.0 56.8 jit_solution(4561848342550816372)
XLA Ops:
  0.0 56.0 %shard_map.73 = bf16[48,48,128]{2,1,0:T(8,128)(2,1)S(1)} custom-call(bf16[48,48,128]{2,1,0:T(8,128)(2,1)} %x_hbm.1, f32[1,128]{1,0:T(1,128)} %bitcast.2, bf16[128,128]{1,0:T(8,128)(2,1)} %left_hbm.1, bf16[128,128]{1,0:T(8,128)(2,1)} %right_hbm.1, f32[1,128]{1,0:T(1,128)} %bitcast.3, bf16[128,128]{1,0:T(8,128)(2,1)} %out_hbm.1, bf16[128,128]{1,0:T(8,128)(2,1)} %gate_hbm.1), custom_call_target="tpu_custom_call" | custom-call | tf_op jit(solution)/shard_map/pallas_call | solution.py:261
  56.0 0.8 %copy.9 = bf16[48,48,128]{2,1,0:T(8,128)(2,1)} copy(bf16[48,48,128]{2,1,0:T(8,128)(2,1)S(1)} %shard_map.73) | data formatting | bytes 1179648

commit v6 on v5

--- a/solution.py
+++ b/solution.py
@@ -28,7 +28,7 @@
     x_hbm, in_gain_hbm, left_hbm, right_hbm, mid_gain_hbm, out_hbm, gate_hbm, o_ref,
     x_ref, in_gain, left_w, right_w, mid_gain, out_w, gate_w,
     weights, ready, wide_r, sent_r, got_r, spread_r, wide_l, sent_l, got_l, spread_l,
-    left, right, sums, outgoing, other, wide_o, sent_o, got_o, spread_o, gates, gain_col,
+    left, right, left_in, right_in, sums, wide_o, sent_o, got_o, spread_o, gates, gain_col,
     load_sem, send_in, recv_in, send_swap, recv_swap, send_out, recv_out,
 ):
     first, second = lax.axis_index("first"), lax.axis_index("second")
@@ -170,42 +170,38 @@
             left[pl.ds(pl.multiple_of(core * 384 + t * 64, 64), 64), lanes] = block[64:128]
         return 0
 
-    def product(target, half, bc):
-        rows = pl.ds(pl.multiple_of(half * 384 + bc * 128, 128), 128)
-        part = jnp.dot(left[rows, :], right[...], preferred_element_type=F32)
+    def swap(source, target, at, i):
+        rows = pl.ds(at, target.shape[0])
+        return pltpu.make_async_remote_copy(
+            src_ref=source.at[rows, :],
+            dst_ref=target,
+            send_sem=send_swap.at[i],
+            recv_sem=recv_swap.at[i],
+            device_id=partner,
+            device_id_type=MESH,
+        )
+
+    def multiply(bc):
+        given = swap(left, left_in.at[pl.ds(bc * 128, 128), :], bc * 128, bc)
+        given.start()
+        part = jnp.dot(left[384 + bc * 128 : 512 + bc * 128, :], right[...], preferred_element_type=F32)
         for zz in range(8):
             for g in range(6):
-                target[g, pl.ds(pl.multiple_of((bc * 8 + zz) * PITCH, 8), 16), :] = part[
+                sums[g, (bc * 8 + zz) * PITCH : (bc * 8 + zz) * PITCH + 16, :] = part[
                     zz * 16 : zz * 16 + 16, g * 128 : g * 128 + 128
                 ]
-
-    def multiply(bc):
-        product(outgoing, 0, bc)
+        if bc == 0:
+            swap(right, right_in, 0, 3).wait_recv()
+        given.wait_recv()
+        part = jnp.dot(left_in[bc * 128 : bc * 128 + 128, :], right_in[...], preferred_element_type=F32)
         for zz in range(8):
-            rows = pl.ds((bc * 8 + zz) * PITCH, 16)
-            pltpu.make_async_remote_copy(
-                src_ref=outgoing.at[:, rows, :],
-                dst_ref=other.at[:, rows, :],
-                send_sem=send_swap.at[bc],
-                recv_sem=recv_swap.at[bc],
-                device_id=partner,
-                device_id_type=MESH,
-            ).start()
-        product(sums, 1, bc)
-
-    third = pl.ds(0, 128)
+            for g in range(6):
+                rows = slice((bc * 8 + zz) * PITCH, (bc * 8 + zz) * PITCH + 16)
+                sums[g, rows, :] = (
+                    sums[g, rows, :] + part[zz * 16 : zz * 16 + 16, g * 128 : g * 128 + 128]
+                ) * 768 ** (-0.5)
 
     def scatter(bc):
-        pltpu.make_async_copy(outgoing.at[:, third, :], other.at[:, third, :], recv_swap.at[bc]).wait()
-
-        def add(g, _):
-            for zz in range(8):
-                rows = pl.ds((bc * 8 + zz) * PITCH, 16)
-                sums[g, rows, :] = (sums[g, rows, :] + other[g, rows, :]) * 768 ** (-0.5)
-            return 0
-
-        lax.fori_loop(0, 6, add, 0, unroll=2)
-
         def step(g, _):
             h, bd = lax.rem(g, 2), lax.div(g, 2)
             for ao in range(2):
@@ -228,11 +224,12 @@
             o_ref[pl.ds(ao * 8, 8), pl.ds(pl.multiple_of(bc * 16, 16), 16), :] = out.astype(BF16).reshape(8, 16, 128)
             return 0
 
-        lax.fori_loop(0, 6, step, 0, unroll=3)
+        lax.fori_loop(0, 6, step, 0, unroll=6)
 
     receive(wide_r, sent_r, got_r, spread_r, recv_in.at[0])
     send_left(2)
     lax.fori_loop(0, 6, gather_right, 0, unroll=2)
+    swap(right, right_in, 0, 3).start()
     for bc in range(3):
         receive(wide_l.at[bc], sent_l.at[bc], got_l.at[bc], spread_l.at[bc], recv_in.at[1 + bc])
         lax.fori_loop(2 * bc, 2 * bc + 2, gather_left, 0, unroll=2)
@@ -248,7 +245,8 @@
     for part in range(3):
         settle(sent_l.at[part], got_l.at[part], send_in.at[1 + part])
         settle(sent_o.at[part], got_o.at[part], send_out.at[part])
-        pltpu.make_async_copy(outgoing.at[:, third, :], other.at[:, third, :], send_swap.at[part]).wait()
+        swap(left, left_in.at[pl.ds(part * 128, 128), :], part * 128, part).wait_send()
+    swap(right, right_in, 0, 3).wait_send()
 
 
 def shards(pair_rows, in_gain, left_weight, right_weight, mid_gain, out_weight, out_gate):
@@ -273,8 +271,8 @@
         + [
             pltpu.VMEM((768, 384), BF16),
             pltpu.VMEM((384, 768), BF16),
-            pltpu.VMEM((6, 24 * PITCH, 128), F32),
-            pltpu.VMEM((6, 24 * PITCH, 128), F32),
+            pltpu.VMEM((384, 384), BF16),
+            pltpu.VMEM((384, 768), BF16),
             pltpu.VMEM((6, 24 * PITCH, 128), F32),
         ]
         + flat(3, 128 * 6)
@@ -282,7 +280,7 @@
             pltpu.VMEM((18, 128, 128), F32),
             pltpu.VMEM((128, 128), F32),
         ]
-        + [pltpu.SemaphoreType.DMA((n,)) for n in (7, 4, 4, 3, 3, 3, 3)],
+        + [pltpu.SemaphoreType.DMA((n,)) for n in (7, 4, 4, 4, 4, 3, 3)],
         compiler_params=pltpu.CompilerParams(
             collective_id=0, has_side_effects=True
         ),

time: 56.9 us -> 56.2 us (0.988)
  Pallas kernels: 56 us -> 55.3 us
    pallas_call x1, Pallas kernels: 56 us -> 55.3 us  [shards(): pl.pallas_call(kernel, out_shape=pltpu.VMEM(pair_rows.shape, BF16), in_sp...]
where the time goes in v6:
time: 56.2 us; the launch traced here: 56.1 us
  Pallas kernels  55.3 us (98%)
  local copies, waits for them, and re-layouts  0.82 us (1%)
    pallas_call x1, Pallas kernels, shards(): pl.pallas_call(kernel, out_shape=pltpu.VMEM(pair_rows.shape, BF16), in_sp...  55.3 us

profile of v6, /device:TPU:1, one launch (start us, length us, event | category | flops | bytes accessed | tf_op | source)
XLA Modules:
  0.0 56.1 jit_solution(1399096983498904445)
XLA Ops:
  0.0 55.3 %shard_map.73 = bf16[48,48,128]{2,1,0:T(8,128)(2,1)S(1)} custom-call(bf16[48,48,128]{2,1,0:T(8,128)(2,1)} %x_hbm.1, f32[1,128]{1,0:T(1,128)} %bitcast.2, bf16[128,128]{1,0:T(8,128)(2,1)} %left_hbm.1, bf16[128,128]{1,0:T(8,128)(2,1)} %right_hbm.1, f32[1,128]{1,0:T(1,128)} %bitcast.3, bf16[128,128]{1,0:T(8,128)(2,1)} %out_hbm.1, bf16[128,128]{1,0:T(8,128)(2,1)} %gate_hbm.1), custom_call_target="tpu_custom_call" | custom-call | tf_op jit(solution)/shard_map/pallas_call | solution.py:259
  55.3 0.8 %copy.9 = bf16[48,48,128]{2,1,0:T(8,128)(2,1)} copy(bf16[48,48,128]{2,1,0:T(8,128)(2,1)S(1)} %shard_map.73) | data formatting | bytes 1179648

commit v7 on v6

--- a/solution.py
+++ b/solution.py
@@ -28,14 +28,16 @@
     x_hbm, in_gain_hbm, left_hbm, right_hbm, mid_gain_hbm, out_hbm, gate_hbm, o_ref,
     x_ref, in_gain, left_w, right_w, mid_gain, out_w, gate_w,
     weights, ready, wide_r, sent_r, got_r, spread_r, wide_l, sent_l, got_l, spread_l,
-    left, right, left_in, right_in, sums, wide_o, sent_o, got_o, spread_o, gates, gain_col,
+    left, right, outbox, inbox, sums, wide_o, sent_o, got_o, spread_o, gates, gain_col,
     load_sem, send_in, recv_in, send_swap, recv_swap, send_out, recv_out,
 ):
     first, second = lax.axis_index("first"), lax.axis_index("second")
     z, core, y, x = lax.div(first, 2), lax.rem(first, 2), lax.div(second, 4), lax.rem(second, 4)
-    me = second * 8 + z
-    partner = (first + 1 - 2 * core, second)
-    layers = [lax.rem(z + dz, 8) for dz in (0, 4, 1, 7, 2, 6, 3, 5)]
+    a_own = lax.rem(z + 8 - core, 8)
+    partner = (lax.rem(z + 1 + 6 * core, 8) * 2 + 1 - core, second)
+    mine = [lax.rem(z + 5 - 5 * core + j, 8) for j in range(4)]
+    theirs = [lax.rem(z + 1 + 3 * core + j, 8) for j in range(4)]
+    near = [lax.rem(z + d, 8) for d in range(8)]
 
     loads = [
         pltpu.make_async_copy(src, dst, load_sem.at[i])
@@ -49,22 +51,25 @@
     for load in loads:
         load.start()
 
-    def each_peer(act):
+    def each_column(act):
         def ahead(i):
             return jnp.where(i == 0, 2, jnp.where(i == 1, 1, jnp.where(i == 2, 3, 0)))
 
-        def column(e, _):
-            ps = lax.rem(y + ahead(lax.div(e, 4)), 4) * 4 + lax.rem(x + ahead(lax.rem(e, 4)), 4)
-            for pz in layers:
-                act(ps * 8 + pz, (pz * 2 + core, ps))
+        def step(e, _):
+            act(lax.rem(y + ahead(lax.div(e, 4)), 4) * 4 + lax.rem(x + ahead(lax.rem(e, 4)), 4), False)
             return 0
 
-        lax.fori_loop(0, 15, column, 0)
-        for pz in layers[1:]:
-            act(second * 8 + pz, (pz * 2 + core, second))
+        lax.fori_loop(0, 15, step, 0)
+        act(second, True)
 
     barrier = pltpu.get_barrier_semaphore()
-    each_peer(lambda chip, device: pl.semaphore_signal(barrier, inc=1, device_id=device, device_id_type=MESH))
+
+    def greet(column, is_own):
+        targets = [(near[d], core) for d in (-3, 3, -2, 2, -1, 1)] + ([] if is_own else [(z, core)])
+        for layer, c in targets + [(layer, 1 - core) for layer in mine]:
+            pl.semaphore_signal(barrier, inc=1, device_id=(layer * 2 + c, column), device_id_type=MESH)
+
+    each_column(greet)
     pl.semaphore_signal(barrier, inc=1, device_id=partner, device_id_type=MESH)
     for load in loads:
         load.wait()
@@ -99,35 +104,54 @@
 
         lax.fori_loop(0, source.shape[0] // 256, step, 0)
 
-    def send(source, target, send_sem, recv_sem):
+    def start(source, target, send_sem, recv_sem, chunk, slot, device):
         rows = source.shape[0] // 128
-
-        def start(chip, device):
-            pltpu.make_async_remote_copy(
-                src_ref=source.at[pl.ds(chip * rows, rows)],
-                dst_ref=target.at[pl.ds(me * rows, rows)],
-                send_sem=send_sem,
-                recv_sem=recv_sem,
-                device_id=device,
-                device_id_type=MESH,
-            ).start()
-
-        each_peer(start)
+        pltpu.make_async_remote_copy(
+            src_ref=source.at[pl.ds(chunk * rows, rows)],
+            dst_ref=target.at[pl.ds(slot * rows, rows)],
+            send_sem=send_sem,
+            recv_sem=recv_sem,
+            device_id=device,
+            device_id_type=MESH,
+        ).start()
+
+    def send(*refs):
+        def act(column, is_own):
+            for o in (7, 3, 4, 0, 2, 5, 1, 6):
+                layer, c = (near[o], 0) if o < 4 else (near[(o + 1) % 8], 1)
+                args = (column * 8 + near[o], second * 8 + o % 4 * 2 + core, (layer * 2 + c, column))
+                if is_own and o in (0, 7):
+                    pl.when(core == (1 if o == 0 else 0))(lambda args=args: start(*refs, *args))
+                else:
+                    start(*refs, *args)
+
+        each_column(act)
+
+    def send_back(*refs):
+        def act(column, is_own):
+            for p in (0, 6, 2, 5, 1, 7, 3, 4):
+                args = (column * 8 + p, second * 8 + a_own, (mine[p // 2] * 2 + p % 2, column))
+                if is_own and p in (1, 6):
+                    pl.when(core == (1 if p == 6 else 0))(lambda args=args: start(*refs, *args))
+                else:
+                    start(*refs, *args)
+
+        each_column(act)
 
     def settle(source, target, sem):
         rows = pl.ds(0, source.shape[0] // 128 * 127)
         pltpu.make_async_copy(source.at[rows], target.at[rows], sem).wait()
 
-    def receive(wide, source, target, spread, sem):
+    def receive(wide, source, target, spread, sem, chunk, slot):
         settle(source, target, sem)
         convert(target, spread)
         rows = source.shape[0] // 128
-        own = wide[pl.ds(me * rows, rows), :]
-        spread[pl.ds(me * rows, rows), :] = own.astype(BF16).astype(F32)
+        own = wide[pl.ds((second * 8 + chunk) * rows, rows), :]
+        spread[pl.ds((second * 8 + slot) * rows, rows), :] = own.astype(BF16).astype(F32)
 
     lax.fori_loop(0, 18, norm, 0, unroll=3)
     convert(wide_r, sent_r)
-    pl.semaphore_wait(barrier, 128)
+    pl.semaphore_wait(barrier, 176)
     send(sent_r, got_r, send_in.at[0], recv_in.at[0])
     lax.fori_loop(0, 6, project, 0)
 
@@ -153,55 +177,48 @@
             right[ao * 64 : ao * 64 + 64, lanes] = jnp.concatenate(swap_blocks(parts), axis=0).astype(BF16)
         return 0
 
-    def gather_left(t, _):
-        bc, h = lax.div(t, 2), lax.rem(t, 2)
-        for pair in range(3):
-            pieces = []
-            for ao in (2 * pair, 2 * pair + 1):
-                pieces += swap_blocks(
-                    [
-                        spread_l[bc, pl.ds((h * 8 + p % 4 * 2 + p // 4) * 48 + ao, 8, stride=6), :]
-                        for p in range(8)
-                    ]
-                )
-            block = jnp.concatenate(pieces, axis=0).astype(BF16).T
-            lanes = slice(pair * 128, pair * 128 + 128)
-            left[pl.ds(pl.multiple_of((1 - core) * 384 + t * 64, 64), 64), lanes] = block[0:64]
-            left[pl.ds(pl.multiple_of(core * 384 + t * 64, 64), 64), lanes] = block[64:128]
-        return 0
-
-    def swap(source, target, at, i):
-        rows = pl.ds(at, target.shape[0])
+    def gather_left(bc):
+        for half, layers in enumerate((theirs, mine)):
+            for pair in range(3):
+                pieces = []
+                for ao in (2 * pair, 2 * pair + 1):
+                    pieces += swap_blocks(
+                        [
+                            spread_l[bc, pl.ds((layers[p // 2] * 2 + p % 2) * 48 + ao, 8, stride=6), :]
+                            for p in range(8)
+                        ]
+                    )
+                block = jnp.concatenate(pieces, axis=0).astype(BF16)
+                left[bc, half * 128 : half * 128 + 128, pair * 128 : pair * 128 + 128] = block.T
+
+    def swap(bc):
         return pltpu.make_async_remote_copy(
-            src_ref=source.at[rows, :],
-            dst_ref=target,
-            send_sem=send_swap.at[i],
-            recv_sem=recv_swap.at[i],
+            src_ref=outbox.at[bc],
+            dst_ref=inbox.at[bc],
+            send_sem=send_swap.at[bc],
+            recv_sem=recv_swap.at[bc],
             device_id=partner,
             device_id_type=MESH,
         )
 
     def multiply(bc):
-        given = swap(left, left_in.at[pl.ds(bc * 128, 128), :], bc * 128, bc)
-        given.start()
-        part = jnp.dot(left[384 + bc * 128 : 512 + bc * 128, :], right[...], preferred_element_type=F32)
+        outbox[bc] = jnp.dot(left[bc, 0:128, :], right[...], preferred_element_type=F32).astype(BF16)
+        swap(bc).start()
+        part = jnp.dot(left[bc, 128:256, :], right[...], preferred_element_type=F32)
         for zz in range(8):
             for g in range(6):
                 sums[g, (bc * 8 + zz) * PITCH : (bc * 8 + zz) * PITCH + 16, :] = part[
                     zz * 16 : zz * 16 + 16, g * 128 : g * 128 + 128
                 ]
-        if bc == 0:
-            swap(right, right_in, 0, 3).wait_recv()
-        given.wait_recv()
-        part = jnp.dot(left_in[bc * 128 : bc * 128 + 128, :], right_in[...], preferred_element_type=F32)
+
+    def scatter(bc):
+        swap(bc).wait_recv()
         for zz in range(8):
             for g in range(6):
                 rows = slice((bc * 8 + zz) * PITCH, (bc * 8 + zz) * PITCH + 16)
-                sums[g, rows, :] = (
-                    sums[g, rows, :] + part[zz * 16 : zz * 16 + 16, g * 128 : g * 128 + 128]
-                ) * 768 ** (-0.5)
-
-    def scatter(bc):
+                there = inbox[bc, zz * 16 : zz * 16 + 16, g * 128 : g * 128 + 128].astype(F32)
+                sums[g, rows, :] = (sums[g, rows, :] + there) * 768 ** (-0.5)
+
         def step(g, _):
             h, bd = lax.rem(g, 2), lax.div(g, 2)
             for ao in range(2):
@@ -226,27 +243,37 @@
 
         lax.fori_loop(0, 6, step, 0, unroll=6)
 
-    receive(wide_r, sent_r, got_r, spread_r, recv_in.at[0])
+    def take(bc):
+        receive(wide_l.at[bc], sent_l.at[bc], got_l.at[bc], spread_l.at[bc], recv_in.at[1 + bc], a_own, core * 7)
+        gather_left(bc)
+        multiply(bc)
+
+    def give(bc):
+        scatter(bc)
+        convert(wide_o.at[bc], sent_o.at[bc])
+        send_back(sent_o.at[bc], got_o.at[bc], send_out.at[bc], recv_out.at[bc])
+
+    receive(wide_r, sent_r, got_r, spread_r, recv_in.at[0], a_own, core * 7)
     send_left(2)
     lax.fori_loop(0, 6, gather_right, 0, unroll=2)
-    swap(right, right_in, 0, 3).start()
-    for bc in range(3):
-        receive(wide_l.at[bc], sent_l.at[bc], got_l.at[bc], spread_l.at[bc], recv_in.at[1 + bc])
-        lax.fori_loop(2 * bc, 2 * bc + 2, gather_left, 0, unroll=2)
-        multiply(bc)
-        scatter(bc)
-        convert(wide_o.at[bc], sent_o.at[bc])
-        send(sent_o.at[bc], got_o.at[bc], send_out.at[bc], recv_out.at[bc])
+    take(0)
+    take(1)
+    give(0)
+    take(2)
+    give(1)
+    give(2)
     for part in range(3):
-        receive(wide_o.at[part], sent_o.at[part], got_o.at[part], spread_o.at[part], recv_out.at[part])
+        receive(
+            wide_o.at[part], sent_o.at[part], got_o.at[part], spread_o.at[part], recv_out.at[part],
+            6 - 5 * core, a_own,
+        )
         finish(part)
 
     settle(sent_r, got_r, send_in.at[0])
     for part in range(3):
         settle(sent_l.at[part], got_l.at[part], send_in.at[1 + part])
         settle(sent_o.at[part], got_o.at[part], send_out.at[part])
-        swap(left, left_in.at[pl.ds(part * 128, 128), :], part * 128, part).wait_send()
-    swap(right, right_in, 0, 3).wait_send()
+        swap(part).wait_send()
 
 
 def shards(pair_rows, in_gain, left_weight, right_weight, mid_gain, out_weight, out_gate):
@@ -269,10 +296,10 @@
         + flat(128 * 18)
         + flat(3, 128 * 6)
         + [
-            pltpu.VMEM((768, 384), BF16),
+            pltpu.VMEM((3, 256, 384), BF16),
             pltpu.VMEM((384, 768), BF16),
-            pltpu.VMEM((384, 384), BF16),
-            pltpu.VMEM((384, 768), BF16),
+            pltpu.VMEM((3, 128, 768), BF16),
+            pltpu.VMEM((3, 128, 768), BF16),
             pltpu.VMEM((6, 24 * PITCH, 128), F32),
         ]
         + flat(3, 128 * 6)
@@ -280,7 +307,7 @@
             pltpu.VMEM((18, 128, 128), F32),
             pltpu.VMEM((128, 128), F32),
         ]
-        + [pltpu.SemaphoreType.DMA((n,)) for n in (7, 4, 4, 4, 4, 3, 3)],
+        + [pltpu.SemaphoreType.DMA((n,)) for n in (7, 4, 4, 3, 3, 3, 3)],
         compiler_params=pltpu.CompilerParams(
             collective_id=0, has_side_effects=True
         ),

time: 56.2 us -> 56.5 us (level)
  no operation moved by 1% of the time
where the time goes in v7:
time: 56.5 us; the launch traced here: 56.4 us
  Pallas kernels  55.6 us (98%)
  local copies, waits for them, and re-layouts  0.82 us (1%)
    pallas_call x1, Pallas kernels, shards(): pl.pallas_call(kernel, out_shape=pltpu.VMEM(pair_rows.shape, BF16), in_sp...  55.6 us

profile of v7, /device:TPU:1, one launch (start us, length us, event | category | flops | bytes accessed | tf_op | source)
XLA Modules:
  0.0 56.4 jit_solution(17172622361059623246)
XLA Ops:
  0.0 55.6 %shard_map.73 = bf16[48,48,128]{2,1,0:T(8,128)(2,1)S(1)} custom-call(bf16[48,48,128]{2,1,0:T(8,128)(2,1)} %x_hbm.1, f32[1,128]{1,0:T(1,128)} %bitcast.2, bf16[128,128]{1,0:T(8,128)(2,1)} %left_hbm.1, bf16[128,128]{1,0:T(8,128)(2,1)} %right_hbm.1, f32[1,128]{1,0:T(1,128)} %bitcast.3, bf16[128,128]{1,0:T(8,128)(2,1)} %out_hbm.1, bf16[128,128]{1,0:T(8,128)(2,1)} %gate_hbm.1), custom_call_target="tpu_custom_call" | custom-call | tf_op jit(solution)/shard_map/pallas_call | solution.py:286
  55.6 0.8 %copy.9 = bf16[48,48,128]{2,1,0:T(8,128)(2,1)} copy(bf16[48,48,128]{2,1,0:T(8,128)(2,1)S(1)} %shard_map.73) | data formatting | bytes 1179648

commit v8 on v7

--- a/solution.py
+++ b/solution.py
@@ -177,19 +177,18 @@
             right[ao * 64 : ao * 64 + 64, lanes] = jnp.concatenate(swap_blocks(parts), axis=0).astype(BF16)
         return 0
 
-    def gather_left(bc):
-        for half, layers in enumerate((theirs, mine)):
-            for pair in range(3):
-                pieces = []
-                for ao in (2 * pair, 2 * pair + 1):
-                    pieces += swap_blocks(
-                        [
-                            spread_l[bc, pl.ds((layers[p // 2] * 2 + p % 2) * 48 + ao, 8, stride=6), :]
-                            for p in range(8)
-                        ]
-                    )
-                block = jnp.concatenate(pieces, axis=0).astype(BF16)
-                left[bc, half * 128 : half * 128 + 128, pair * 128 : pair * 128 + 128] = block.T
+    def gather_left(bc, half, layers):
+        for pair in range(3):
+            pieces = []
+            for ao in (2 * pair, 2 * pair + 1):
+                pieces += swap_blocks(
+                    [
+                        spread_l[bc, pl.ds((layers[p // 2] * 2 + p % 2) * 48 + ao, 8, stride=6), :]
+                        for p in range(8)
+                    ]
+                )
+            block = jnp.concatenate(pieces, axis=0).astype(BF16)
+            left[bc, half * 128 : half * 128 + 128, pair * 128 : pair * 128 + 128] = block.T
 
     def swap(bc):
         return pltpu.make_async_remote_copy(
@@ -202,8 +201,10 @@
         )
 
     def multiply(bc):
+        gather_left(bc, 0, theirs)
         outbox[bc] = jnp.dot(left[bc, 0:128, :], right[...], preferred_element_type=F32).astype(BF16)
         swap(bc).start()
+        gather_left(bc, 1, mine)
         part = jnp.dot(left[bc, 128:256, :], right[...], preferred_element_type=F32)
         for zz in range(8):
             for g in range(6):
@@ -245,7 +246,6 @@
 
     def take(bc):
         receive(wide_l.at[bc], sent_l.at[bc], got_l.at[bc], spread_l.at[bc], recv_in.at[1 + bc], a_own, core * 7)
-        gather_left(bc)
         multiply(bc)
 
     def give(bc):
@@ -256,12 +256,10 @@
     receive(wide_r, sent_r, got_r, spread_r, recv_in.at[0], a_own, core * 7)
     send_left(2)
     lax.fori_loop(0, 6, gather_right, 0, unroll=2)
-    take(0)
-    take(1)
-    give(0)
-    take(2)
-    give(1)
-    give(2)
+    for bc in range(3):
+        take(bc)
+    for bc in range(3):
+        give(bc)
     for part in range(3):
         receive(
             wide_o.at[part], sent_o.at[part], got_o.at[part], spread_o.at[part], recv_out.at[part],

time: 56.5 us -> 55.2 us (0.977)
  Pallas kernels: 55.6 us -> 54.3 us
    pallas_call x1, Pallas kernels: 55.6 us -> 54.3 us  [shards(): pl.pallas_call(kernel, out_shape=pltpu.VMEM(pair_rows.shape, BF16), in_sp...]
where the time goes in v8:
time: 55.2 us; the launch traced here: 55.1 us
  Pallas kernels  54.3 us (98%)
  local copies, waits for them, and re-layouts  0.82 us (1%)
    pallas_call x1, Pallas kernels, shards(): pl.pallas_call(kernel, out_shape=pltpu.VMEM(pair_rows.shape, BF16), in_sp...  54.3 us

profile of v8, /device:TPU:1, one launch (start us, length us, event | category | flops | bytes accessed | tf_op | source)
XLA Modules:
  0.0 55.1 jit_solution(6570950227843542992)
XLA Ops:
  0.0 54.3 %shard_map.73 = bf16[48,48,128]{2,1,0:T(8,128)(2,1)S(1)} custom-call(bf16[48,48,128]{2,1,0:T(8,128)(2,1)} %x_hbm.1, f32[1,128]{1,0:T(1,128)} %bitcast.2, bf16[128,128]{1,0:T(8,128)(2,1)} %left_hbm.1, bf16[128,128]{1,0:T(8,128)(2,1)} %right_hbm.1, f32[1,128]{1,0:T(1,128)} %bitcast.3, bf16[128,128]{1,0:T(8,128)(2,1)} %out_hbm.1, bf16[128,128]{1,0:T(8,128)(2,1)} %gate_hbm.1), custom_call_target="tpu_custom_call" | custom-call | tf_op jit(solution)/shard_map/pallas_call | solution.py:284
  54.3 0.8 %copy.9 = bf16[48,48,128]{2,1,0:T(8,128)(2,1)} copy(bf16[48,48,128]{2,1,0:T(8,128)(2,1)S(1)} %shard_map.73) | data formatting | bytes 1179648

commit v9 on v8

--- a/solution.py
+++ b/solution.py
@@ -28,7 +28,7 @@
     x_hbm, in_gain_hbm, left_hbm, right_hbm, mid_gain_hbm, out_hbm, gate_hbm, o_ref,
     x_ref, in_gain, left_w, right_w, mid_gain, out_w, gate_w,
     weights, ready, wide_r, sent_r, got_r, spread_r, wide_l, sent_l, got_l, spread_l,
-    left, right, outbox, inbox, sums, wide_o, sent_o, got_o, spread_o, gates, gain_col,
+    left, right, outbox, inbox, sums, wide_o, sent_o, got_o, spread_o, wide_p, sent_p, got_p, spread_p, gates, gain_col,
     load_sem, send_in, recv_in, send_swap, recv_swap, send_out, recv_out,
 ):
     first, second = lax.axis_index("first"), lax.axis_index("second")
@@ -220,6 +220,9 @@
                 there = inbox[bc, zz * 16 : zz * 16 + 16, g * 128 : g * 128 + 128].astype(F32)
                 sums[g, rows, :] = (sums[g, rows, :] + there) * 768 ** (-0.5)
 
+        wide, skip = (wide_o, 0) if bc < 2 else (wide_p, 4)
+        count = wide.shape[0] // 128
+
         def step(g, _):
             h, bd = lax.rem(g, 2), lax.div(g, 2)
             for ao in range(2):
@@ -227,50 +230,54 @@
                     sums[g, pl.ds(bc * 8 * PITCH + ao * 8 + a8, 8, stride=PITCH), :] for a8 in range(8)
                 ]
                 for p, part in enumerate(swap_blocks(parts)):
-                    wide_o[bc, pl.ds((h * 8 + p) * 48 + ao * 3 + bd, 8, stride=6), :] = part
+                    at = (h * 8 + p) * 8 * count + (2 * bc + ao - skip) * 3 + bd
+                    wide[pl.ds(at, 8, stride=count), :] = part
             return 0
 
         lax.fori_loop(0, 6, step, 0, unroll=3)
 
-    def finish(part):
+    def finish(spread, skip):
+        count = spread.shape[0] // 128
+
         def step(r, _):
-            v = spread_o[part, pl.ds(r, 128, stride=6), :]
+            v = spread[pl.ds(r, 128, stride=count), :]
             v = v - jnp.mean(v, axis=0, keepdims=True)
             v = v * lax.rsqrt(jnp.mean(v * v, axis=0, keepdims=True) + 1e-05) * gain_col[...]
-            out = jnp.dot(v.astype(BF16).T, out_w[...], preferred_element_type=F32) * gates[part * 6 + r]
-            ao, bc = part * 2 + lax.div(r, 3), lax.rem(r, 3)
+            out = jnp.dot(v.astype(BF16).T, out_w[...], preferred_element_type=F32) * gates[skip * 3 + r]
+            ao, bc = skip + lax.div(r, 3), lax.rem(r, 3)
             o_ref[pl.ds(ao * 8, 8), pl.ds(pl.multiple_of(bc * 16, 16), 16), :] = out.astype(BF16).reshape(8, 16, 128)
             return 0
 
-        lax.fori_loop(0, 6, step, 0, unroll=6)
+        lax.fori_loop(0, count, step, 0, unroll=6)
 
     def take(bc):
         receive(wide_l.at[bc], sent_l.at[bc], got_l.at[bc], spread_l.at[bc], recv_in.at[1 + bc], a_own, core * 7)
         multiply(bc)
 
-    def give(bc):
-        scatter(bc)
-        convert(wide_o.at[bc], sent_o.at[bc])
-        send_back(sent_o.at[bc], got_o.at[bc], send_out.at[bc], recv_out.at[bc])
+    def give(wide, sent, got, i):
+        convert(wide, sent)
+        send_back(sent, got, send_out.at[i], recv_out.at[i])
 
     receive(wide_r, sent_r, got_r, spread_r, recv_in.at[0], a_own, core * 7)
     send_left(2)
     lax.fori_loop(0, 6, gather_right, 0, unroll=2)
     for bc in range(3):
         take(bc)
-    for bc in range(3):
-        give(bc)
-    for part in range(3):
-        receive(
-            wide_o.at[part], sent_o.at[part], got_o.at[part], spread_o.at[part], recv_out.at[part],
-            6 - 5 * core, a_own,
-        )
-        finish(part)
+    scatter(0)
+    scatter(1)
+    give(wide_o, sent_o, got_o, 0)
+    scatter(2)
+    give(wide_p, sent_p, got_p, 1)
+    receive(wide_o, sent_o, got_o, spread_o, recv_out.at[0], 6 - 5 * core, a_own)
+    finish(spread_o, 0)
+    receive(wide_p, sent_p, got_p, spread_p, recv_out.at[1], 6 - 5 * core, a_own)
+    finish(spread_p, 4)
 
     settle(sent_r, got_r, send_in.at[0])
+    settle(sent_o, got_o, send_out.at[0])
+    settle(sent_p, got_p, send_out.at[1])
     for part in range(3):
         settle(sent_l.at[part], got_l.at[part], send_in.at[1 + part])
-        settle(sent_o.at[part], got_o.at[part], send_out.at[part])
         swap(part).wait_send()
 
 
@@ -300,12 +307,13 @@
             pltpu.VMEM((3, 128, 768), BF16),
             pltpu.VMEM((6, 24 * PITCH, 128), F32),
         ]
-        + flat(3, 128 * 6)
+        + flat(128 * 12)
+        + flat(128 * 6)
         + [
             pltpu.VMEM((18, 128, 128), F32),
             pltpu.VMEM((128, 128), F32),
         ]
-        + [pltpu.SemaphoreType.DMA((n,)) for n in (7, 4, 4, 3, 3, 3, 3)],
+        + [pltpu.SemaphoreType.DMA((n,)) for n in (7, 4, 4, 3, 3, 2, 2)],
         compiler_params=pltpu.CompilerParams(
             collective_id=0, has_side_effects=True
         ),

time: 55.2 us -> 54.5 us (0.987)
  Pallas kernels: 54.3 us -> 53.6 us
    pallas_call x1, Pallas kernels: 54.3 us -> 53.6 us  [shards(): pl.pallas_call(kernel, out_shape=pltpu.VMEM(pair_rows.shape, BF16), in_sp...]
where the time goes in v9:
time: 54.5 us
  Pallas kernels  53.6 us (98%)
  local copies, waits for them, and re-layouts  0.82 us (2%)
    pallas_call x1, Pallas kernels, shards(): pl.pallas_call(kernel, out_shape=pltpu.VMEM(pair_rows.shape, BF16), in_sp...  53.6 us

profile of v9, /device:TPU:1, one launch (start us, length us, event | category | flops | bytes accessed | tf_op | source)
XLA Modules:
  0.0 54.5 jit_solution(7998556208676307007)
XLA Ops:
  0.0 53.6 %shard_map.73 = bf16[48,48,128]{2,1,0:T(8,128)(2,1)S(1)} custom-call(bf16[48,48,128]{2,1,0:T(8,128)(2,1)} %x_hbm.1, f32[1,128]{1,0:T(1,128)} %bitcast.2, bf16[128,128]{1,0:T(8,128)(2,1)} %left_hbm.1, bf16[128,128]{1,0:T(8,128)(2,1)} %right_hbm.1, f32[1,128]{1,0:T(1,128)} %bitcast.3, bf16[128,128]{1,0:T(8,128)(2,1)} %out_hbm.1, bf16[128,128]{1,0:T(8,128)(2,1)} %gate_hbm.1), custom_call_target="tpu_custom_call" | custom-call | tf_op jit(solution)/shard_map/pallas_call | solution.py:291
  53.6 0.8 %copy.9 = bf16[48,48,128]{2,1,0:T(8,128)(2,1)} copy(bf16[48,48,128]{2,1,0:T(8,128)(2,1)S(1)} %shard_map.73) | data formatting | bytes 1179648

commit v10 on v9

--- a/solution.py
+++ b/solution.py
@@ -200,10 +200,12 @@
             device_id_type=MESH,
         )
 
-    def multiply(bc):
+    def multiply_theirs(bc):
         gather_left(bc, 0, theirs)
         outbox[bc] = jnp.dot(left[bc, 0:128, :], right[...], preferred_element_type=F32).astype(BF16)
         swap(bc).start()
+
+    def multiply_mine(bc):
         gather_left(bc, 1, mine)
         part = jnp.dot(left[bc, 128:256, :], right[...], preferred_element_type=F32)
         for zz in range(8):
@@ -252,7 +254,7 @@
 
     def take(bc):
         receive(wide_l.at[bc], sent_l.at[bc], got_l.at[bc], spread_l.at[bc], recv_in.at[1 + bc], a_own, core * 7)
-        multiply(bc)
+        multiply_theirs(bc)
 
     def give(wide, sent, got, i):
         convert(wide, sent)
@@ -263,9 +265,12 @@
     lax.fori_loop(0, 6, gather_right, 0, unroll=2)
     for bc in range(3):
         take(bc)
+        if bc < 2:
+            multiply_mine(bc)
     scatter(0)
     scatter(1)
     give(wide_o, sent_o, got_o, 0)
+    multiply_mine(2)
     scatter(2)
     give(wide_p, sent_p, got_p, 1)
     receive(wide_o, sent_o, got_o, spread_o, recv_out.at[0], 6 - 5 * core, a_own)

time: 54.5 us -> 54.5 us (level)
  no operation moved by 1% of the time
where the time goes in v10:
time: 54.5 us
  Pallas kernels  53.6 us (98%)
  local copies, waits for them, and re-layouts  0.82 us (2%)
    pallas_call x1, Pallas kernels, shards(): pl.pallas_call(kernel, out_shape=pltpu.VMEM(pair_rows.shape, BF16), in_sp...  53.6 us

profile of v10, /device:TPU:1, one launch (start us, length us, event | category | flops | bytes accessed | tf_op | source)
XLA Modules:
  0.0 54.5 jit_solution(41668369730790741)
XLA Ops:
  0.0 53.6 %shard_map.73 = bf16[48,48,128]{2,1,0:T(8,128)(2,1)S(1)} custom-call(bf16[48,48,128]{2,1,0:T(8,128)(2,1)} %x_hbm.1, f32[1,128]{1,0:T(1,128)} %bitcast.2, bf16[128,128]{1,0:T(8,128)(2,1)} %left_hbm.1, bf16[128,128]{1,0:T(8,128)(2,1)} %right_hbm.1, f32[1,128]{1,0:T(1,128)} %bitcast.3, bf16[128,128]{1,0:T(8,128)(2,1)} %out_hbm.1, bf16[128,128]{1,0:T(8,128)(2,1)} %gate_hbm.1), custom_call_target="tpu_custom_call" | custom-call | tf_op jit(solution)/shard_map/pallas_call | solution.py:296
  53.6 0.8 %copy.9 = bf16[48,48,128]{2,1,0:T(8,128)(2,1)} copy(bf16[48,48,128]{2,1,0:T(8,128)(2,1)S(1)} %shard_map.73) | data formatting | bytes 1179648

commit v11 on v9

--- a/solution.py
+++ b/solution.py
@@ -151,9 +151,9 @@
 
     lax.fori_loop(0, 18, norm, 0, unroll=3)
     convert(wide_r, sent_r)
+    lax.fori_loop(0, 6, project, 0)
     pl.semaphore_wait(barrier, 176)
     send(sent_r, got_r, send_in.at[0], recv_in.at[0])
-    lax.fori_loop(0, 6, project, 0)
 
     def send_left(bc):
         convert(wide_l.at[bc], sent_l.at[bc])

time: 54.5 us -> 54.7 us (level)
  no operation moved by 1% of the time
where the time goes in v11:
time: 54.7 us; the launch traced here: 54.6 us
  Pallas kernels  53.8 us (98%)
  local copies, waits for them, and re-layouts  0.82 us (1%)
    pallas_call x1, Pallas kernels, shards(): pl.pallas_call(kernel, out_shape=pltpu.VMEM(pair_rows.shape, BF16), in_sp...  53.8 us

profile of v11, /device:TPU:1, one launch (start us, length us, event | category | flops | bytes accessed | tf_op | source)
XLA Modules:
  0.0 54.6 jit_solution(6628735592506657773)
XLA Ops:
  0.0 53.8 %shard_map.73 = bf16[48,48,128]{2,1,0:T(8,128)(2,1)S(1)} custom-call(bf16[48,48,128]{2,1,0:T(8,128)(2,1)} %x_hbm.1, f32[1,128]{1,0:T(1,128)} %bitcast.2, bf16[128,128]{1,0:T(8,128)(2,1)} %left_hbm.1, bf16[128,128]{1,0:T(8,128)(2,1)} %right_hbm.1, f32[1,128]{1,0:T(1,128)} %bitcast.3, bf16[128,128]{1,0:T(8,128)(2,1)} %out_hbm.1, bf16[128,128]{1,0:T(8,128)(2,1)} %gate_hbm.1), custom_call_target="tpu_custom_call" | custom-call | tf_op jit(solution)/shard_map/pallas_call | solution.py:291
  53.8 0.8 %copy.9 = bf16[48,48,128]{2,1,0:T(8,128)(2,1)} copy(bf16[48,48,128]{2,1,0:T(8,128)(2,1)S(1)} %shard_map.73) | data formatting | bytes 1179648
